TPU v7x, 256 devices: a whole 4x4x8 slice. The times are simulated.
256 devices in a mesh: dp: 32 (over x, z_lo, y), chan: 8 (over z_hi, core).
Axes of the slice: x: 4, y: 4, z: 8 (z_hi: 4, z_lo: 2; z = z_hi * 2 + z_lo), core: 2. Of those that a mesh axis runs over, the one named last changes fastest.
Arguments:
- patches: bfloat16 [256, 256, 1280], P('dp', None, 'chan'), may hold values from -13 to 13
- cotangent: bfloat16 [256, 256, 1280], P('dp', None, 'chan'), may hold values from -33 to 33
- w_token_in: bfloat16 [640, 256], replicated, may hold values from -0.375 to 0.375
- b_token_in: float32 [640], replicated, may hold values from -3 to 3
- w_token_out: bfloat16 [256, 640], replicated, may hold values from -0.25 to 0.25
- layer_norm_gain: float32 [1280], replicated, may hold values from 0.25 to 1.75
- layer_norm_bias: float32 [1280], replicated, may hold values from -3 to 3
Outputs:
- grad_patches: bfloat16 [256, 256, 1280], P('dp', None, 'chan')
- grad_w_in: float32 [640, 256], replicated
- grad_w_out: float32 [256, 640], replicated
- grad_b_in: float32 [640], replicated
- grad_gain: float32 [1280], P('chan')
- grad_shift: float32 [1280], P('chan')
All inputs are finite; a program needn't handle non-finite values.
Results may differ from a plain program's by a relative error of at most 0.0065.
Values may be sent and summed in bfloat16 or wider, within the bound.
A program may use at most 64 MiB of HBM per device.

v0:
```python
import math

import jax
import jax.numpy as jnp
from jax import lax
from jax.sharding import PartitionSpec as P

CHANNEL_COUNT = 1280


eps_norm = 1e-05


def from_everyone(shard, axis):
    copies = jnp.broadcast_to(shard, (lax.axis_size(axis), *shard.shape))
    return lax.all_to_all(copies, axis, split_axis=0, concat_axis=0, tiled=True)


def taken_together(shard, axis):
    return from_everyone(shard, axis).sum(axis=0)


def together(arrays, axis):
    ends = [0]
    for a in arrays:
        ends.append(ends[-1] + a.size)
    so_far = taken_together(jnp.concatenate([a.ravel() for a in arrays]), axis)
    return tuple((so_far[b:e].reshape(a.shape) for a, b, e in zip(arrays, ends, ends[1:])))


def together_2(arrays, axis):
    flat, at, outs = (jnp.concatenate([a.reshape(-1) for a in arrays]), 0, [])
    so_far = lax.psum(flat, axis)
    for a in arrays:
        outs.append(so_far[at : at + a.size].reshape(a.shape))
        at += a.size
    return tuple(outs)


def total_of_pieces(shard, axis):
    return lax.all_gather(shard, axis).sum(0)


def shards(
    patches, cotangent, w_token_in, b_token_in, w_token_out, layer_norm_gain, layer_norm_bias
):
    where = lax.axis_index("chan")
    local_width = patches.shape[2]
    images = float(patches.shape[0] * lax.axis_size("dp"))
    input_float = patches.astype(jnp.float32)
    totals = together((jnp.sum(input_float, -1), jnp.sum(input_float * input_float, -1)), "chan")
    row_average = totals[0] / CHANNEL_COUNT
    inverse_deviation = lax.rsqrt(totals[1] / CHANNEL_COUNT - row_average * row_average + eps_norm)
    local_gain = lax.dynamic_slice_in_dim(layer_norm_gain, where * local_width, local_width, 0)
    local_bias = lax.dynamic_slice_in_dim(layer_norm_bias, where * local_width, local_width, 0)
    centered_input = (input_float - row_average[..., None]) * inverse_deviation[..., None]
    normalized_output = (centered_input * local_gain + local_bias).astype(jnp.bfloat16)
    pre = (
        jnp.einsum("kp,bpc->bkc", w_token_in, normalized_output, preferred_element_type=jnp.float32)
        + b_token_in[None, :, None]
    )
    cdf = 0.5 * (1.0 + jax.scipy.special.erf(pre / math.sqrt(2.0)))
    act = (pre * cdf).astype(jnp.bfloat16)
    slope = cdf + pre * jnp.exp(-0.5 * pre * pre) / math.sqrt(2.0 * math.pi)
    grad_act = jnp.einsum("pk,bpc->bkc", w_token_out, cotangent, preferred_element_type=jnp.float32)
    grad_pre = (grad_act * slope).astype(jnp.bfloat16)
    gradient_normalized = jnp.einsum(
        "kp,bkc->bpc", w_token_in, grad_pre, preferred_element_type=jnp.float32
    ).astype(jnp.bfloat16)
    dw_out = jnp.einsum("bpc,bkc->pk", cotangent, act, preferred_element_type=jnp.float32)
    dw_in = jnp.einsum(
        "bkc,bpc->kp", grad_pre, normalized_output, preferred_element_type=jnp.float32
    )
    db_in = jnp.sum(grad_pre.astype(jnp.float32), axis=(0, 2))
    summed = together_2((dw_in, dw_out, db_in), ("dp", "chan"))
    gradient_block = gradient_normalized.astype(jnp.float32)
    norm_terms = together(
        (
            jnp.sum(gradient_block * centered_input, axis=(0, 1)),
            jnp.sum(gradient_block, axis=(0, 1)),
        ),
        "dp",
    )
    gradient_centered = gradient_block * local_gain
    sums = (
        total_of_pieces(jnp.sum(gradient_centered, -1), "chan"),
        total_of_pieces(jnp.sum(gradient_centered * centered_input, -1), "chan"),
    )
    first_term = sums[0] / CHANNEL_COUNT
    second_term = sums[1] / CHANNEL_COUNT
    result = cotangent.astype(jnp.float32) + inverse_deviation[..., None] * (
        gradient_centered - first_term[..., None] - centered_input * second_term[..., None]
    )
    grad_patches = result.astype(jnp.bfloat16)
    return (
        grad_patches,
        summed[0] / images,
        summed[1] / images,
        summed[2] / images,
        norm_terms[0] / images,
        norm_terms[1] / images,
    )


def solution(mesh):
    placed = (P("dp", None, "chan"), P("dp", None, "chan"), P(), P(), P(), P(), P())
    return jax.shard_map(
        shards,
        mesh=mesh,
        in_specs=placed,
        out_specs=(P("dp", None, "chan"), P(), P(), P(), P("chan"), P("chan")),
        check_vma=False,
    )
```

profile of v0, /device:TPU:1, one launch (start us, length us, event | category | flops | bytes accessed | tf_op | source)
XLA Modules:
  0.0 305.5 jit_solution(11005699022924083191)
XLA Ops:
  7.2 0.0 copy-start
  7.2 0.0 copy-start.1
  7.2 1.4 convert_reduce_fusion.1
  8.6 0.7 broadcast_in_dim.4
  9.3 10.0 %all-to-all-start = ((f32[8,1,4096]{2,1,0:T(1,128)}), f32[8,1,4096]{2,1,0:T(1,128)S(1)}, u32[]{:S(2)}, u32[]{:S(2)}) async-start(f32[8,1,4096]{2,1,0:T(1,128)} %broadcast_in_dim.4), calls=%async_computation | async-start | bytes 262144 | tf_op jit(solution)/shard_map/all_to_all | solution.py:16
  19.3 0.0 all-reduce.2.cloned.1.call-start
  19.3 0.8 dynamic_slice.6
  20.1 0.8 dynamic_slice.7
  20.8 6.5 %all-to-all-done = f32[8,1,4096]{2,1,0:T(1,128)S(1)} async-done(((f32[8,1,4096]{2,1,0:T(1,128)}), f32[8,1,4096]{2,1,0:T(1,128)S(1)}, u32[]{:S(2)}, u32[]{:S(2)}) %all-to-all-start) | async-done | bytes 131104 | tf_op jit(solution)/shard_map/all_to_all | solution.py:16
  27.3 0.1 reduce_sum.101
  27.5 0.0 copy-done
  27.5 0.0 copy-done.1
  27.5 0.0 copy-start.2
  27.5 0.0 copy-start.5
  27.5 0.7 fusion.34
  28.3 0.3 copy-done.2
  28.6 0.0 copy-done.5
  28.6 0.0 copy-start.4
  28.6 0.9 fusion.30
  29.5 0.1 copy-done.4
  29.6 1.8 convert_reduce_fusion
  31.4 1.6 convolution_bitcast_fusion
  33.0 0.9 fusion.23
  33.9 0.2 copy.16
  34.2 1.4 copy.26
  35.6 1.2 pad_maximum_fusion
  36.8 0.0 copy-start.3
  36.8 0.0 all-reduce.2.cloned.1.call-update
  36.9 0.2 convert_reduce_fusion.2
  37.0 0.1 pad_maximum_fusion.2
  37.1 0.7 broadcast_in_dim.5
  37.8 7.5 %all-to-all-start.1 = ((f32[32,1,320]{2,1,0:T(1,128)}), f32[32,1,320]{2,1,0:T(1,128)S(1)}, u32[]{:S(2)}, u32[]{:S(2)}) async-start(f32[32,1,320]{2,1,0:T(1,128)} %broadcast_in_dim.5), calls=%async_computation.1 | async-start | bytes 98304 | tf_op jit(solution)/shard_map/all_to_all | solution.py:16
  45.3 16.2 %all-gather.1 = f32[64,256]{1,0:T(8,128)S(1)} all-gather(f32[8,256]{1,0:T(8,128)S(1)} %get-tuple-element.7), channel_id=3, replica_groups=mesh['dp'=32,'chan'=8] {'chan'}, dimensions={0}, use_global_device_ids=true | all-gather | bytes 73728 | tf_op jit(solution)/shard_map/all_gather | solution.py:41
  61.5 14.6 %all-gather = f32[64,256]{1,0:T(8,128)S(1)} all-gather(f32[8,256]{1,0:T(8,128)S(1)} %get-tuple-element.8), channel_id=2, replica_groups=mesh['dp'=32,'chan'=8] {'chan'}, dimensions={0}, use_global_device_ids=true | all-gather | bytes 73728 | tf_op jit(solution)/shard_map/all_gather | solution.py:41
  76.1 0.0 copy-done.3
  76.1 1.4 fusion.21
  77.5 0.0 all-to-all-done.1
  77.5 0.1 reduce_sum.109
  77.5 0.6 slice_multiply_fusion.5
  78.2 215.8 %all-reduce.2.cloned.1.call-done = f32[328320]{0:T(1024)} async-done(((f32[328320]{0:T(1024)}), f32[328320]{0:T(1024)}) %all-reduce.2.cloned.1.call-update) | async-done | bytes 1313296 | tf_op jit(solution)/shard_map/psum | solution.py:33
  294.0 1.4 slice_multiply_fusion
  295.4 1.0 div.68
  296.3 1.0 div.66
  297.3 1.3 slice_multiply_fusion.4
  (12 shorter events, 0.1 us)
Async XLA Ops:
  7.2 20.3 %copy-start = (bf16[640,256]{1,0:T(8,128)(2,1)S(1)}, bf16[640,256]{1,0:T(8,128)(2,1)}, u32[]{:S(2)}) copy-start(bf16[640,256]{1,0:T(8,128)(2,1)} %param.9) | copy-start | bytes 983044
  7.2 20.3 %copy-start.1 = (bf16[8,256,160]{1,2,0:T(8,128)(2,1)S(1)}, bf16[8,256,160]{1,2,0:T(8,128)(2,1)}, u32[]{:S(2)}) copy-start(bf16[8,256,160]{1,2,0:T(8,128)(2,1)} %param.7) | copy-start | bytes 1966084
  9.3 18.0 %all-to-all-start = ((f32[8,1,4096]{2,1,0:T(1,128)}), f32[8,1,4096]{2,1,0:T(1,128)S(1)}, u32[]{:S(2)}, u32[]{:S(2)}) async-start(f32[8,1,4096]{2,1,0:T(1,128)} %broadcast_in_dim.4), calls=%async_computation | async-start | bytes 262144 | tf_op jit(solution)/shard_map/all_to_all | solution.py:16
  19.3 274.7 %all-reduce.2.cloned.1.call-start = ((), (), s32[]{:S(2)}) async-start(), calls=%async_computation.2 | async-start | bytes 2629632 | tf_op jit(solution)/shard_map/psum | solution.py:33
  27.5 1.1 copy-start.2
  27.5 1.1 copy-start.5
  28.6 1.0 copy-start.4
  36.8 39.3 %copy-start.3 = (bf16[8,256,160]{1,2,0:T(8,128)(2,1)S(1)}, bf16[8,256,160]{1,2,0:T(8,128)(2,1)}, u32[]{:S(2)}) copy-start(bf16[8,256,160]{1,2,0:T(8,128)(2,1)} %param.8) | copy-start | bytes 1966084
  37.8 39.7 %all-to-all-start.1 = ((f32[32,1,320]{2,1,0:T(1,128)}), f32[32,1,320]{2,1,0:T(1,128)S(1)}, u32[]{:S(2)}, u32[]{:S(2)}) async-start(f32[32,1,320]{2,1,0:T(1,128)} %broadcast_in_dim.5), calls=%async_computation.1 | async-start | bytes 98304 | tf_op jit(solution)/shard_map/all_to_all | solution.py:16
Sparse Core Ops, SparseCore 0:
  37.0 256.9 all-reduce.1
where the time goes:
time: 306 us; the launch traced here: 305 us
  waiting for transfers between devices  222 us (73%)
  blocking collectives  30.8 us (10%)
  starting transfers between devices  17.5 us (6%)
  between operations  14.2 us (5%)
  other arithmetic  7.67 us (3%)
  local copies, waits for them, and re-layouts  7.04 us (2%)
  matrix products  5.99 us (2%)
    psum x1, waiting for transfers between devices, together_2(): so_far = lax.psum(flat, axis)  216 us
    all_gather x2, blocking collectives, total_of_pieces(): return lax.all_gather(shard, axis).sum(0)  30.8 us
    all_to_all x2, starting transfers between devices, from_everyone(): return lax.all_to_all(copies, axis, split_axis=0, concat_axis=0, tiled=True)  17.4 us
    all_to_all x2, waiting for transfers between devices, from_everyone(): return lax.all_to_all(copies, axis, split_axis=0, concat_axis=0, tiled=True)  6.49 us
  transfers between devices with their start and end apart: 3, of which 2 were waited for; matrix products, arithmetic and copies ran while one was open for 1% of the time, Pallas kernels for 0%

commit v1 on v0

--- a/solution.py
+++ b/solution.py
@@ -3,42 +3,159 @@
 import jax
 import jax.numpy as jnp
 from jax import lax
+from jax.experimental import pallas as pl
+from jax.experimental.pallas import tpu as pltpu
 from jax.sharding import PartitionSpec as P
 
 CHANNEL_COUNT = 1280
-
-
+MESH = pl.DeviceIdType.MESH
 eps_norm = 1e-05
 
 
 def from_everyone(shard, axis):
     copies = jnp.broadcast_to(shard, (lax.axis_size(axis), *shard.shape))
     return lax.all_to_all(copies, axis, split_axis=0, concat_axis=0, tiled=True)
-
-
-def taken_together(shard, axis):
-    return from_everyone(shard, axis).sum(axis=0)
 
 
 def together(arrays, axis):
     ends = [0]
     for a in arrays:
         ends.append(ends[-1] + a.size)
-    so_far = taken_together(jnp.concatenate([a.ravel() for a in arrays]), axis)
+    so_far = from_everyone(jnp.concatenate([a.ravel() for a in arrays]), axis).sum(axis=0)
     return tuple((so_far[b:e].reshape(a.shape) for a, b, e in zip(arrays, ends, ends[1:])))
 
 
-def together_2(arrays, axis):
-    flat, at, outs = (jnp.concatenate([a.reshape(-1) for a in arrays]), 0, [])
-    so_far = lax.psum(flat, axis)
-    for a in arrays:
-        outs.append(so_far[at : at + a.size].reshape(a.shape))
-        at += a.size
-    return tuple(outs)
-
-
-def total_of_pieces(shard, axis):
-    return lax.all_gather(shard, axis).sum(0)
+def remote(src, dst, send, recv, dev):
+    return pltpu.make_async_remote_copy(
+        src_ref=src, dst_ref=dst, send_sem=send, recv_sem=recv, device_id=dev, device_id_type=MESH
+    )
+
+
+def place():
+    dp, ch = lax.axis_index("dp"), lax.axis_index("chan")
+    x, zl, y = dp // 8, (dp // 4) % 2, dp % 4
+    zh, core = ch // 2, ch % 2
+    return x, y, zh * 2 + zl, core
+
+
+def device(x, y, z, core):
+    return (x * 8 + (z % 2) * 4 + y, (z // 2) * 2 + core)
+
+
+def reduce_kernel(
+    g_ref, small_ref, full_ref, sum_ref, r0, s, r1, t, r2, sm1, smt, sm2, sm3, sm4,
+    s0, q0, s1, q1, s2, q2, s3, q3, s4, q4, a1, b1, a2, b2, a3, b3,
+):
+    x, y, z, core = place()
+    other = 1 - core
+    q = x * 4 + y
+    partner = device(x, y, z, other)
+
+    def plane(j):
+        xx, yy = (x + j // 4) % 4, (y + j % 4) % 4
+        return device(xx, yy, z, core), xx * 4 + yy
+
+    def column(d):
+        return device(x, y, (z + d) % 8, core)
+
+    barrier = pltpu.get_barrier_semaphore()
+    for dev in [partner] + [plane(j)[0] for j in range(1, 16)] + [column(d) for d in range(1, 8)]:
+        pl.semaphore_signal(barrier, inc=1, device_id=dev, device_id_type=MESH)
+    pl.semaphore_wait(barrier, 23)
+
+    sends = []
+    c0 = remote(g_ref.at[other], r0, s0, q0, partner)
+    c0.start()
+    for j in range(1, 16):
+        c = remote(small_ref, sm1.at[j], a1.at[j], b1, plane(j)[0])
+        c.start()
+        sends.append(c)
+    c0.wait_recv()
+    for i in range(16):
+        s[i] = (g_ref[core, i].astype(jnp.float32) + r0[i].astype(jnp.float32)).astype(jnp.bfloat16)
+    for j in range(1, 16):
+        dev, qq = plane(j)
+        c = remote(s.at[qq], r1.at[j], s1.at[j], q1, dev)
+        c.start()
+        sends.append(c)
+    pltpu.make_async_copy(sm1.at[pl.ds(1, 15)], sm1.at[pl.ds(1, 15)], b1).wait()
+    acc = small_ref[...]
+    for j in range(1, 16):
+        acc = acc + sm1[j]
+    smt[...] = acc
+    for d in range(1, 8):
+        c = remote(smt, sm2.at[d], a2.at[d], b2, column(d))
+        c.start()
+        sends.append(c)
+    pltpu.make_async_copy(r1.at[pl.ds(1, 15)], r1.at[pl.ds(1, 15)], q1).wait()
+    acc = s[q].astype(jnp.float32)
+    for j in range(1, 16):
+        acc = acc + r1[j].astype(jnp.float32)
+    t[...] = acc.astype(jnp.bfloat16)
+    for d in range(1, 8):
+        c = remote(t, r2.at[d], s2.at[d], q2, column(d))
+        c.start()
+        sends.append(c)
+    pltpu.make_async_copy(sm2.at[pl.ds(1, 7)], sm2.at[pl.ds(1, 7)], b2).wait()
+    near = smt[...] + sm2[7 - 6 * (z % 2)]
+    acc = smt[...]
+    for d in range(1, 8):
+        acc = acc + sm2[d]
+    sm3[...] = acc
+    c = remote(sm3, sm4, a3, b3, partner)
+    c.start()
+    sends.append(c)
+    pltpu.make_async_copy(r2.at[pl.ds(1, 7)], r2.at[pl.ds(1, 7)], q2).wait()
+    acc = t[...].astype(jnp.float32)
+    for d in range(1, 8):
+        acc = acc + r2[d].astype(jnp.float32)
+    full_ref[core, q] = acc.astype(jnp.bfloat16)
+    arrive = []
+    for j in range(1, 16):
+        c = remote(full_ref.at[core, q], full_ref.at[core, q], s3.at[j], q3.at[j], plane(j)[0])
+        c.start()
+        sends.append(c)
+    for j in range(0, 16):
+        xx, yy = (x + 4 - j // 4) % 4, (y + 4 - j % 4) % 4
+        qq = xx * 4 + yy
+        if j:
+            pltpu.make_async_copy(full_ref.at[core, qq], full_ref.at[core, qq], q3.at[j]).wait()
+        c = remote(full_ref.at[core, qq], full_ref.at[core, qq], s4.at[j], q4, partner)
+        c.start()
+        sends.append(c)
+    pltpu.make_async_copy(sm4, sm4, b3).wait()
+    row = lax.broadcasted_iota(jnp.int32, (8, 128), 0)
+    sum_ref[...] = jnp.where(row < 5, sm3[...] + sm4[...], near)
+    pltpu.make_async_copy(full_ref.at[other], full_ref.at[other], q4).wait()
+    c0.wait_send()
+    for c in sends:
+        c.wait_send()
+
+
+def reduce_all(g, small):
+    b16, f32, dma = jnp.bfloat16, jnp.float32, pltpu.SemaphoreType.DMA
+    vmem = pl.BlockSpec(memory_space=pltpu.VMEM)
+    return pl.pallas_call(
+        reduce_kernel,
+        out_shape=(jax.ShapeDtypeStruct((2, 16, 16, 640), b16), jax.ShapeDtypeStruct((8, 128), f32)),
+        in_specs=[vmem, vmem],
+        out_specs=(vmem, vmem),
+        scratch_shapes=[
+            pltpu.VMEM((16, 16, 640), b16),
+            pltpu.VMEM((16, 16, 640), b16),
+            pltpu.VMEM((16, 16, 640), b16),
+            pltpu.VMEM((16, 640), b16),
+            pltpu.VMEM((8, 16, 640), b16),
+            pltpu.VMEM((16, 8, 128), f32),
+            pltpu.VMEM((8, 128), f32),
+            pltpu.VMEM((8, 8, 128), f32),
+            pltpu.VMEM((8, 128), f32),
+            pltpu.VMEM((8, 128), f32),
+            dma, dma, dma((16,)), dma, dma((8,)), dma, dma((16,)), dma((16,)), dma((16,)), dma,
+            dma((16,)), dma, dma((8,)), dma, dma, dma,
+        ],
+        compiler_params=pltpu.CompilerParams(collective_id=0, has_side_effects=True),
+    )(g, small)
 
 
 def shards(
@@ -68,38 +185,32 @@
         "kp,bkc->bpc", w_token_in, grad_pre, preferred_element_type=jnp.float32
     ).astype(jnp.bfloat16)
     dw_out = jnp.einsum("bpc,bkc->pk", cotangent, act, preferred_element_type=jnp.float32)
-    dw_in = jnp.einsum(
-        "bkc,bpc->kp", grad_pre, normalized_output, preferred_element_type=jnp.float32
-    )
+    dw_in = jnp.einsum("bkc,bpc->pk", grad_pre, normalized_output, preferred_element_type=jnp.float32)
     db_in = jnp.sum(grad_pre.astype(jnp.float32), axis=(0, 2))
-    summed = together_2((dw_in, dw_out, db_in), ("dp", "chan"))
     gradient_block = gradient_normalized.astype(jnp.float32)
-    norm_terms = together(
-        (
+    flat = jnp.concatenate(
+        [
+            db_in,
             jnp.sum(gradient_block * centered_input, axis=(0, 1)),
             jnp.sum(gradient_block, axis=(0, 1)),
-        ),
-        "dp",
-    )
+            jnp.zeros((64,), jnp.float32),
+        ]
+    )
+    weights = jnp.stack([dw_in, dw_out]).astype(jnp.bfloat16).reshape(2, 16, 16, 640)
+    full, sums = reduce_all(weights, flat.reshape(8, 128))
+    full = full.reshape(2, 256, 640).astype(jnp.float32) / images
+    sums = sums.reshape(-1) / images
     gradient_centered = gradient_block * local_gain
-    sums = (
-        total_of_pieces(jnp.sum(gradient_centered, -1), "chan"),
-        total_of_pieces(jnp.sum(gradient_centered * centered_input, -1), "chan"),
-    )
-    first_term = sums[0] / CHANNEL_COUNT
-    second_term = sums[1] / CHANNEL_COUNT
+    first, second = together(
+        (jnp.sum(gradient_centered, -1), jnp.sum(gradient_centered * centered_input, -1)), "chan"
+    )
+    first_term = first / CHANNEL_COUNT
+    second_term = second / CHANNEL_COUNT
     result = cotangent.astype(jnp.float32) + inverse_deviation[..., None] * (
         gradient_centered - first_term[..., None] - centered_input * second_term[..., None]
     )
     grad_patches = result.astype(jnp.bfloat16)
-    return (
-        grad_patches,
-        summed[0] / images,
-        summed[1] / images,
-        summed[2] / images,
-        norm_terms[0] / images,
-        norm_terms[1] / images,
-    )
+    return grad_patches, full[0].T, full[1], sums[:640], sums[640:800], sums[800:960]
 
 
 def solution(mesh):

time: 306 us -> 78.6 us (0.26)
  waiting for transfers between devices: 222 us -> 10.4 us
  Pallas kernels: 0 us -> 32.1 us
  blocking collectives: 30.8 us -> 0 us
  between operations: 14.2 us -> 0.84 us
    psum x1 -> x0, waiting for transfers between devices: 216 us -> none  [together_2(): so_far = lax.psum(flat, axis)]
    pallas_call x0 -> x1, Pallas kernels: none -> 32.1 us  [reduce_all(): pl.pallas_call(reduce_kernel, out_shape=(jax.ShapeDtypeStruct((2, 16, 16,...]
    all_gather x2 -> x0, blocking collectives: 30.8 us -> none  [total_of_pieces(): return lax.all_gather(shard, axis).sum(0)]
    all_to_all x2, waiting for transfers between devices: 6.49 us -> 10.4 us  [from_everyone(): return lax.all_to_all(copies, axis, split_axis=0, concat_axis=0, tiled=True)]
  transfers between devices with their start and end apart: 3 -> 2, of which waited for: 2 -> 2; matrix products, arithmetic and copies ran while one was open for 1% -> 8% of each run, Pallas kernels for 0% -> 0%
where the time goes in v1:
time: 78.6 us; the launch traced here: 78.1 us
  Pallas kernels  32.1 us (41%)
  starting transfers between devices  16 us (20%)
  waiting for transfers between devices  10.4 us (13%)
  local copies, waits for them, and re-layouts  6.6 us (8%)
  other arithmetic  6.57 us (8%)
  matrix products  5.54 us (7%)
  between operations  0.84 us (1%)
    pallas_call x1, Pallas kernels, reduce_all(): pl.pallas_call(reduce_kernel, out_shape=(jax.ShapeDtypeStruct((2, 16, 16,...  32.1 us
    all_to_all x2, starting transfers between devices, from_everyone(): return lax.all_to_all(copies, axis, split_axis=0, concat_axis=0, tiled=True)  16 us
    all_to_all x2, waiting for transfers between devices, from_everyone(): return lax.all_to_all(copies, axis, split_axis=0, concat_axis=0, tiled=True)  10.4 us
    dot_general x1, matrix products, shards(): jnp.einsum('pk,bpc->bkc', w_token_out, cotangent, preferred_element_type=...  1.9 us
  transfers between devices with their start and end apart: 2, of which 2 were waited for; matrix products, arithmetic and copies ran while one was open for 8% of the time, Pallas kernels for 0%

profile of v1, /device:TPU:1, one launch (start us, length us, event | category | flops | bytes accessed | tf_op | source)
XLA Modules:
  0.0 78.1 jit_solution(9878583945788355842)
XLA Ops:
  0.6 0.0 copy-start
  0.6 0.0 copy-start.1
  0.7 1.4 %convert_reduce_fusion.1 = (f32[8,256]{1,0:T(8,128)S(1)}, f32[8,256]{1,0:T(8,128)S(1)}) fusion(bf16[8,256,160]{1,2,0:T(8,128)(2,1)} %param.7), kind=kLoop, calls=%fused_computation.16 | loop fusion | flops 1306624 | bytes 671744 | tf_op jit(solution)/shard_map/reduce_sum | solution.py:168
  2.1 0.7 broadcast_in_dim.6
  2.8 10.0 %all-to-all-start = ((f32[8,1,4096]{2,1,0:T(1,128)}), f32[8,1,4096]{2,1,0:T(1,128)S(1)}, u32[]{:S(2)}, u32[]{:S(2)}) async-start(f32[8,1,4096]{2,1,0:T(1,128)} %broadcast_in_dim.6), calls=%async_computation | async-start | bytes 262144 | tf_op jit(solution)/shard_map/all_to_all | solution.py:17
  12.7 0.8 dynamic_slice.6
  13.5 0.8 dynamic_slice.7
  14.3 6.5 %all-to-all-done = f32[8,1,4096]{2,1,0:T(1,128)S(1)} async-done(((f32[8,1,4096]{2,1,0:T(1,128)}), f32[8,1,4096]{2,1,0:T(1,128)S(1)}, u32[]{:S(2)}, u32[]{:S(2)}) %all-to-all-start) | async-done | bytes 131104 | tf_op jit(solution)/shard_map/all_to_all | solution.py:17
  20.8 0.1 reduce_sum.83
  20.9 0.0 copy-done
  20.9 0.0 copy-done.1
  20.9 0.0 copy-start.2
  21.0 0.0 copy-start.4
  21.0 0.7 fusion.38
  21.7 0.3 copy-done.2
  22.0 0.0 copy-done.4
  22.0 0.0 copy-start.3
  22.0 1.1 %fusion.34 = bf16[640,256]{0,1:T(8,128)(2,1)S(1)} fusion(bf16[8,256,160]{1,2,0:T(8,128)(2,1)S(1)} %copy-done.2, f32[8,160,640]{2,1,0:T(8,128)S(1)} %fusion.38, f32[640]{0:T(1024)S(1)} %copy-done.4), kind=kOutput, calls=%fused_computation.43 | convolution fusion | flops 424509440 | bytes 4262400 | tf_op jit(solution)/shard_map/bpc,bkc->pk/dot_general | solution.py:187
  23.2 0.0 copy-done.3
  23.2 1.9 %convert_reduce_fusion = (f32[640]{0:T(1024)S(1)}, bf16[8,640,160]{1,2,0:T(8,128)(2,1)S(1)}) fusion(f32[8,160,640]{2,1,0:T(8,128)S(1)} %fusion.38, f32[640]{0:T(1024)S(1)} %copy-done.4, bf16[8,256,160]{1,2,0:T(8,128)(2,1)S(1)} %copy-done.2, bf16[256,640]{1,0:T(8,128)(2,1)S(1)} %copy-done.3), kind=kOutput, calls=%fused_computation.13 | convolution fusion | flops 430079360 | bytes 5903360 | tf_op jit(solution)/shard_map/pk,bpc->bkc/dot_general | solution.py:182
  25.1 0.9 %fusion.33 = bf16[256,640]{1,0:T(8,128)(2,1)S(1)} fusion(bf16[8,640,160]{1,2,0:T(8,128)(2,1)S(1)} %get-tuple-element.27, bf16[8,256,160]{1,2,0:T(8,128)(2,1)S(1)} %copy-done.1, f32[160]{0:T(256)S(1)} %dynamic_slice.7, f32[160]{0:T(256)S(1)} %dynamic_slice.6, f32[8,256]{1,0:T(8,128)S(1)} %div.49, f32[8,256]{1,0:T(8,128)S(1)} %add_rsqrt_fusion), kind=kOutput, calls=%fused_computation.42 | convolution fusion | flops 421560320 | bytes 2639104 | tf_op jit(solution)/shard_map/bkc,bpc->pk/dot_general | solution.py:188
  25.9 0.9 %fusion.23 = (f32[160]{0:T(256)S(1)}, f32[8,256]{1,0:T(8,128)S(1)}, f32[8,256]{1,0:T(8,128)S(1)}, bf16[8,160,256]{2,1,0:T(8,128)(2,1)S(1)}) fusion(bf16[8,256,160]{1,2,0:T(8,128)(2,1)S(1)} %copy-done.1, f32[8,256]{1,0:T(8,128)S(1)} %div.49, f32[8,256]{1,0:T(8,128)S(1)} %add_rsqrt_fusion, f32[160]{0:T(256)S(1)} %dynamic_slice.6, ...), kind=kOutput, calls=%fused_computation.32 | convolution fusion | flops 423030624 | bytes 3310848 | tf_op jit(solution)/shard_map/kp,bkc->bpc/dot_general | solution.py:184
  26.9 0.2 convert_reduce_fusion.2
  27.1 0.9 %pad_maximum_fusion.g_ref = bf16[2,16,16,640]{3,2,1,0:T(8,128)(2,1)} fusion(bf16[1,16,16,640]{3,2,1,0:T(8,128)(2,1)S(1)} %bitcast.96, bf16[1,16,16,640]{3,2,1,0:T(8,128)(2,1)S(1)} %bitcast.97), kind=kLoop, calls=%fused_computation.44 | loop fusion | flops 327680 | bytes 1310720 | tf_op jit(solution)/shard_map/stack | solution.py:199
  28.0 0.7 maximum_bitcast_fusion.small_ref
  28.7 32.1 %shard_map.118 = (bf16[2,16,16,640]{3,2,1,0:T(8,128)(2,1)}, f32[8,128]{1,0:T(8,128)}) custom-call(bf16[2,16,16,640]{3,2,1,0:T(8,128)(2,1)} %pad_maximum_fusion.g_ref, f32[8,128]{1,0:T(8,128)} %maximum_bitcast_fusion.small_ref), custom_call_target="tpu_custom_call" | custom-call | tf_op jit(solution)/shard_map/pallas_call | solution.py:138
  60.8 0.7 fusion.41
  61.4 0.7 broadcast_in_dim.7
  62.2 6.1 %all-to-all-start.1 = ((f32[8,1,4096]{2,1,0:T(1,128)}), f32[8,1,4096]{2,1,0:T(1,128)S(1)}, u32[]{:S(2)}, u32[]{:S(2)}) async-start(f32[8,1,4096]{2,1,0:T(1,128)} %broadcast_in_dim.7), calls=%async_computation.1 | async-start | bytes 262144 | tf_op jit(solution)/shard_map/all_to_all | solution.py:17
  68.2 1.2 %convert_multiply_fusion.1 = f32[2,16,16,640]{3,2,1,0:T(8,128)S(1)} fusion(bf16[2,16,16,640]{3,2,1,0:T(8,128)(2,1)} %get-tuple-element.8), kind=kLoop, calls=%fused_computation.39 | loop fusion | flops 655360 | bytes 1966080 | tf_op jit(solution)/shard_map/div | solution.py:201
  69.4 0.9 %fusion.45 = (f32[1,16,16,640]{3,2,1,0:T(8,128)}, f32[1,16,16,640]{3,2,1,0:T(8,128)S(1)}) fusion(f32[2,16,16,640]{3,2,1,0:T(8,128)S(1)} %convert_multiply_fusion.1), kind=kLoop, calls=%fused_computation.60 | loop fusion | bytes 2621440 | tf_op jit(solution)/shard_map/slice | solution.py:213
  70.4 0.6 fusion.46
  71.0 1.1 %copy.17 = f32[256,640]{0,1:T(8,128)} copy(f32[256,640]{1,0:T(8,128)S(1)} %bitcast.93) | data formatting | bytes 1310720 | tf_op jit(solution)/shard_map/squeeze | solution.py:213
  72.1 0.6 slice_bitcast_fusion
  72.7 3.9 %all-to-all-done.1 = f32[8,1,4096]{2,1,0:T(1,128)S(1)} async-done(((f32[8,1,4096]{2,1,0:T(1,128)}), f32[8,1,4096]{2,1,0:T(1,128)S(1)}, u32[]{:S(2)}, u32[]{:S(2)}) %all-to-all-start.1) | async-done | bytes 131104 | tf_op jit(solution)/shard_map/all_to_all | solution.py:17
  76.6 0.1 reduce_sum.86
  76.7 1.4 %fusion.22 = bf16[8,256,160]{1,2,0:T(8,128)(2,1)} fusion(bf16[8,160,256]{2,1,0:T(8,128)(2,1)S(1)} %get-tuple-element.25, bf16[8,256,160]{1,2,0:T(8,128)(2,1)S(1)} %copy-done.1, bf16[8,256,160]{1,2,0:T(8,128)(2,1)S(1)} %copy-done.2, f32[8,256]{1,0:T(8,128)S(1)} %div.57, f32[8,256]{1,0:T(8,128)S(1)} %div.55, f32[160]{0:T(256)S(1)} %dynamic_slice.6, ...), kind=kLoop, calls=%fused_computation.31 | loop fusion | flops 3932160 | bytes 2654848 | tf_op jit(solution)/shard_map/convert_element_type | solution.py:212
  (14 shorter events, 0.1 us)
Async XLA Ops:
  0.6 20.3 %copy-start = (bf16[640,256]{1,0:T(8,128)(2,1)S(1)}, bf16[640,256]{1,0:T(8,128)(2,1)}, u32[]{:S(2)}) copy-start(bf16[640,256]{1,0:T(8,128)(2,1)} %param.9) | copy-start | bytes 983044
  0.6 20.3 %copy-start.1 = (bf16[8,256,160]{1,2,0:T(8,128)(2,1)S(1)}, bf16[8,256,160]{1,2,0:T(8,128)(2,1)}, u32[]{:S(2)}) copy-start(bf16[8,256,160]{1,2,0:T(8,128)(2,1)} %param.7) | copy-start | bytes 1966084
  2.8 18.0 %all-to-all-start = ((f32[8,1,4096]{2,1,0:T(1,128)}), f32[8,1,4096]{2,1,0:T(1,128)S(1)}, u32[]{:S(2)}, u32[]{:S(2)}) async-start(f32[8,1,4096]{2,1,0:T(1,128)} %broadcast_in_dim.6), calls=%async_computation | async-start | bytes 262144 | tf_op jit(solution)/shard_map/all_to_all | solution.py:17
  20.9 1.1 %copy-start.2 = (bf16[8,256,160]{1,2,0:T(8,128)(2,1)S(1)}, bf16[8,256,160]{1,2,0:T(8,128)(2,1)}, u32[]{:S(2)}) copy-start(bf16[8,256,160]{1,2,0:T(8,128)(2,1)} %param.8) | copy-start | bytes 1966084
  21.0 1.1 %copy-start.4 = (f32[640]{0:T(1024)S(1)}, f32[640]{0:T(1024)}, u32[]{:S(2)}) copy-start(f32[640]{0:T(1024)} %param.10) | copy-start | bytes 7684
  22.0 1.1 %copy-start.3 = (bf16[256,640]{1,0:T(8,128)(2,1)S(1)}, bf16[256,640]{1,0:T(8,128)(2,1)}, u32[]{:S(2)}) copy-start(bf16[256,640]{1,0:T(8,128)(2,1)} %param.11) | copy-start | bytes 983044
  62.2 14.4 %all-to-all-start.1 = ((f32[8,1,4096]{2,1,0:T(1,128)}), f32[8,1,4096]{2,1,0:T(1,128)S(1)}, u32[]{:S(2)}, u32[]{:S(2)}) async-start(f32[8,1,4096]{2,1,0:T(1,128)} %broadcast_in_dim.7), calls=%async_computation.1 | async-start | bytes 262144 | tf_op jit(solution)/shard_map/all_to_all | solution.py:17

commit v2 on v0

v2 whole, which is shorter than its diff:
```python
import math

import jax
import jax.numpy as jnp
from jax import lax
from jax.experimental import pallas as pl
from jax.experimental.pallas import tpu as pltpu
from jax.sharding import PartitionSpec as P

CHANNELS = 1280
PATCH = 256
HID = 640
LOCAL = 160
IMG = 8
WIDE = IMG * LOCAL
IMAGES = 256
MESH = pl.DeviceIdType.MESH
eps_norm = 1e-05
F32, BF16 = jnp.float32, jnp.bfloat16


def remote(src, dst, send, recv, dev):
    return pltpu.make_async_remote_copy(
        src_ref=src, dst_ref=dst, send_sem=send, recv_sem=recv, device_id=dev, device_id_type=MESH
    )


def arrived(ref, sem):
    pltpu.make_async_copy(ref, ref, sem).wait()


def place():
    dp, ch = lax.axis_index("dp"), lax.axis_index("chan")
    x, zl, y = dp // 8, (dp // 4) % 2, dp % 4
    zh, core = ch // 2, ch % 2
    return x, y, zh * 2 + zl, core


def device(x, y, z, core):
    return (x * 8 + (z % 2) * 4 + y, (z // 2) * 2 + core)


def dot(a, b):
    return jnp.dot(a, b, preferred_element_type=F32)


def dot_nt(a, b):
    return lax.dot_general(a, b, (((1,), (1,)), ((), ())), preferred_element_type=F32)


def picks(r, j, which):
    b = ((r >> 3) & 1) * 4 + (r & 3)
    return (((r >> 2) & 1) == which) & (j >= b * LOCAL) & (j < b * LOCAL + LOCAL)


def halves(v):
    hi = v.astype(BF16)
    return hi, (v - hi.astype(F32)).astype(BF16)


def row_totals(stats):
    return jnp.transpose(stats)[:16]


def columns(v):
    hi = v.astype(BF16).astype(F32)
    mid = (v - hi).astype(BF16).astype(F32)
    low = v - hi - mid
    stacked = jnp.concatenate([hi, mid, low, jnp.zeros((80, PATCH), F32)], axis=0)
    return jnp.transpose(stacked).astype(BF16)


def kernel(
    x_hbm, g_hbm, win_hbm, wout_hbm, b_ref, gain_ref, bias_ref,
    out_ref, dwin_ref, dwout_ref, db_ref, norm_ref,
    xv, gv, win, wout, winT, woutT, xc, left, right, ga, xh, rs, gn, bcol, gb, sel, spread,
    e_src, e_in, e_sum, e_far, f_src, f_in, f_sum, f_far,
    grads, r0, s, r1, t, r2, full, small, sm1, smt, sm2, sm3, sm4,
    ld, es, eq1, eq2, fs, fq1, fq2, s0, q0, s1, q1, s2, q2, s3, q3, s4, q4, a1, b1, a2, b2, a3, b3,
):
    x, y, z, core = place()
    other = 1 - core
    q = x * 4 + y
    partner = device(x, y, z, other)
    sends = []

    def start(c):
        c.start()
        sends.append(c)

    def plane(j):
        xx, yy = (x + j // 4) % 4, (y + j % 4) % 4
        return device(xx, yy, z, core), xx * 4 + yy

    def column(d, c=core):
        return device(x, y, (z + d) % 8, c)

    loads = [
        pltpu.make_async_copy(a, b, ld.at[i])
        for i, (a, b) in enumerate(((x_hbm, xv), (g_hbm, gv), (wout_hbm, wout), (win_hbm, win)))
    ]
    for c in loads:
        c.start()

    barrier = pltpu.get_barrier_semaphore()
    peers = [partner] + [plane(j)[0] for j in range(1, 16)] + [column(d) for d in range(1, 8)]
    peers += [column(d, other) for d in (2, 4, 6)]
    for dev in peers:
        pl.semaphore_signal(barrier, inc=1, device_id=dev, device_id_type=MESH)

    j = lax.broadcasted_iota(jnp.int32, (WIDE, 128), 0)
    r = lax.broadcasted_iota(jnp.int32, (WIDE, 128), 1)
    for which in range(2):
        sel[which] = jnp.where((r < 16) & picks(r, j, which), 1.0, 0.0).astype(BF16)
    r = lax.broadcasted_iota(jnp.int32, (128, WIDE), 0)
    j = lax.broadcasted_iota(jnp.int32, (128, WIDE), 1)
    for which in range(2):
        spread[which] = jnp.where((r < 48) & picks(r, j, which), 1.0, 0.0).astype(BF16)

    def total(first, second):
        hi, low = halves(second)
        return first, dot(hi, sel[1]) + dot(low, sel[1])

    loads[0].wait()
    for b in range(IMG):
        xc[:, pl.ds(b * LOCAL, LOCAL)] = xv[b]
    xf = xc[...].astype(F32)
    hi, low = halves(xf * xf)
    e_src[...] = row_totals(dot(xc[...], sel[0]) + dot(hi, sel[1]) + dot(low, sel[1]))
    pl.semaphore_wait(barrier, len(peers))
    start(remote(e_src, e_in, es.at[0], eq1, partner))

    loads[1].wait()
    for b in range(IMG):
        left[1, :, pl.ds(b * LOCAL, LOCAL)] = gv[b]
    loads[2].wait()
    woutT[...] = jnp.transpose(wout[...])

    def second_step(src, came, summed, far, sem1, send, sem2):
        arrived(came, sem1)
        both = src[...] + came[...]
        summed[0] = both[:8]
        summed[1] = both[8:]
        n = 1
        for d in (2, 4, 6):
            for c in (core, other):
                start(remote(summed.at[core], far.at[d // 2 - 1, core], send.at[n], sem2, column(d, c)))
                n += 1

    def finish(summed, far, sem2):
        arrived(far, sem2)
        tot = summed[...] + far[0] + far[1] + far[2]
        return tot * (1.0 / CHANNELS)

    second_step(e_src, e_in, e_sum, e_far, eq1, es, eq2)

    ga[...] = dot(woutT[...], left[1])
    loads[3].wait()
    winT[...] = jnp.transpose(win[...])
    bcol[...] = jnp.transpose(jnp.broadcast_to(b_ref[...], (128, HID)))
    where = z // 2 * 2 + core
    for i, ref in enumerate((gain_ref, bias_ref)):
        mine = ref[pl.ds(where, 1), :]
        for b in range(IMG):
            gb[pl.ds(i, 1), pl.ds(b * LOCAL, LOCAL)] = mine

    mean_sq = finish(e_sum, e_far, eq2)
    rows = []
    for h in range(2):
        mean = mean_sq[h, :4]
        rows += [mean, lax.rsqrt(mean_sq[h, 4:] - mean * mean + eps_norm)]
    cols = columns(jnp.concatenate(rows, axis=0))
    rs[...] = dot(cols, spread[1])
    xhat = (xc[...].astype(F32) - dot(cols, spread[0])) * rs[...]
    xh[...] = xhat
    left[0] = (xhat * gb[0:1, :] + gb[1:2, :]).astype(BF16)

    for k in range(0, HID, 128):
        ks = pl.ds(k, 128)
        pre = dot(win[ks, :], left[0]) + bcol[ks, 0:1]
        cdf = 0.5 * (1.0 + lax.erf(pre * (1.0 / math.sqrt(2.0))))
        right[1, ks, :] = (pre * cdf).astype(BF16)
        slope = cdf + pre * jnp.exp(-0.5 * pre * pre) * (1.0 / math.sqrt(2.0 * math.pi))
        right[0, ks, :] = (ga[ks, :] * slope).astype(BF16)

    grads[other] = dot_nt(left[other], right[other]).astype(BF16).reshape(16, 16, HID)
    start(remote(grads.at[other], r0, s0, q0, partner))
    grads[core] = dot_nt(left[core], right[core]).astype(BF16).reshape(16, 16, HID)
    arrived(r0, q0)
    for i in range(16):
        s[i] = (grads[core, i].astype(F32) + r0[i].astype(F32)).astype(BF16)
    for j in range(1, 16):
        dev, qq = plane(j)
        start(remote(s.at[qq], r1.at[j], s1.at[j], q1, dev))

    gn[...] = dot(winT[...], right[0]).astype(BF16)
    gnf = gn[...].astype(F32)
    along = gnf * xh[...]
    gain = gb[0:1, :]
    hi1, low1 = halves(gnf * gain)
    hi2, low2 = halves(along * gain)
    f_src[...] = row_totals(
        dot(hi1, sel[0]) + dot(low1, sel[0]) + dot(hi2, sel[1]) + dot(low2, sel[1])
    )
    start(remote(f_src, f_in, fs.at[0], fq1, partner))

    db = dot_nt(jnp.ones((8, WIDE), BF16), right[0])[0:1]
    by_channel = [jnp.sum(v, axis=0, keepdims=True) for v in (along, gnf)]
    for i in range(5):
        small[pl.ds(i, 1), :] = db[:, i * 128 : i * 128 + 128]
    for i, v in enumerate(by_channel):
        one = v[:, :LOCAL]
        for b in range(1, IMG):
            one = one + v[:, b * LOCAL : b * LOCAL + LOCAL]
        small[pl.ds(5 + i, 1), :] = one[:, :128]
        small[pl.ds(7, 1), pl.ds(32 * i, 32)] = one[:, 128:]
    small[pl.ds(7, 1), pl.ds(64, 64)] = jnp.zeros((1, 64), F32)
    for j in range(1, 16):
        start(remote(small, sm1.at[j], a1.at[j], b1, plane(j)[0]))

    second_step(f_src, f_in, f_sum, f_far, fq1, fs, fq2)

    arrived(r1.at[pl.ds(1, 15)], q1)
    acc = s[q].astype(F32)
    for j in range(1, 16):
        acc = acc + r1[j].astype(F32)
    t[...] = acc.astype(BF16)
    for d in range(1, 8):
        start(remote(t, r2.at[d], s2.at[d], q2, column(d)))

    means = finish(f_sum, f_far, fq2)
    cols = columns(means.reshape(16, PATCH))
    inner = gn[...].astype(F32) * gb[0:1, :] - dot(cols, spread[0]) - xh[...] * dot(cols, spread[1])
    res = (left[1].astype(F32) + rs[...] * inner).astype(BF16)
    for b in range(IMG):
        out_ref[b] = res[:, b * LOCAL : b * LOCAL + LOCAL]

    arrived(r2.at[pl.ds(1, 7)], q2)
    acc = t[...].astype(F32)
    for d in range(1, 8):
        acc = acc + r2[d].astype(F32)
    full[core, q] = acc.astype(BF16)
    for j in range(1, 16):
        start(remote(full.at[core, q], full.at[core, q], s3.at[j], q3.at[j], plane(j)[0]))
    start(remote(full.at[core, q], full.at[core, q], s4.at[0], q4, partner))

    arrived(sm1.at[pl.ds(1, 15)], b1)
    acc = small[...]
    for j in range(1, 16):
        acc = acc + sm1[j]
    smt[...] = acc
    for d in range(1, 8):
        start(remote(smt, sm2.at[d], a2.at[d], b2, column(d)))

    for j in range(1, 16):
        xx, yy = (x + 4 - j // 4) % 4, (y + 4 - j % 4) % 4
        qq = xx * 4 + yy
        arrived(full.at[core, qq], q3.at[j])
        start(remote(full.at[core, qq], full.at[core, qq], s4.at[j], q4, partner))

    arrived(sm2.at[pl.ds(1, 7)], b2)
    near = smt[...] + sm2[7 - 6 * (z % 2)]
    acc = smt[...]
    for d in range(1, 8):
        acc = acc + sm2[d]
    sm3[...] = acc
    start(remote(sm3, sm4, a3, b3, partner))
    arrived(full.at[other], q4)
    arrived(sm4, b3)
    scale = 1.0 / IMAGES
    dwin_ref[...] = jnp.transpose(full[0].reshape(PATCH, HID).astype(F32) * scale)
    dwout_ref[...] = full[1].reshape(PATCH, HID).astype(F32) * scale
    db = (sm3[...] + sm4[...]) * scale
    for i in range(5):
        db_ref[:, pl.ds(i * 128, 128)] = db[i : i + 1, :]
    near = near * scale
    for i in range(2):
        norm_ref[pl.ds(i, 1), pl.ds(0, 128)] = near[5 + i : 6 + i, :]
        norm_ref[pl.ds(i, 1), pl.ds(128, 32)] = near[7:8, 32 * i : 32 * i + 32]
    for c in sends:
        c.wait_send()


def shards(patches, cotangent, w_in, b_in, w_out, gain, bias):
    dma = pltpu.SemaphoreType.DMA
    vmem = pl.BlockSpec(memory_space=pltpu.VMEM)
    hbm = pl.BlockSpec(memory_space=pltpu.HBM)

    def buf(dtype, *shape):
        return pltpu.VMEM(shape, dtype)

    out, dwin, dwout, db, norm = pl.pallas_call(
        kernel,
        out_shape=(
            jax.ShapeDtypeStruct((IMG, PATCH, LOCAL), BF16),
            jax.ShapeDtypeStruct((HID, PATCH), F32),
            jax.ShapeDtypeStruct((PATCH, HID), F32),
            jax.ShapeDtypeStruct((1, HID), F32),
            jax.ShapeDtypeStruct((2, LOCAL), F32),
        ),
        in_specs=[hbm, hbm, hbm, hbm, vmem, vmem, vmem],
        out_specs=(vmem,) * 5,
        scratch_shapes=[
            buf(BF16, IMG, PATCH, LOCAL),
            buf(BF16, IMG, PATCH, LOCAL),
            buf(BF16, HID, PATCH),
            buf(BF16, PATCH, HID),
            buf(BF16, PATCH, HID),
            buf(BF16, HID, PATCH),
            buf(BF16, PATCH, WIDE),
            buf(BF16, 2, PATCH, WIDE),
            buf(BF16, 2, HID, WIDE),
            buf(F32, HID, WIDE),
            buf(F32, PATCH, WIDE),
            buf(F32, PATCH, WIDE),
            buf(BF16, PATCH, WIDE),
            buf(F32, HID, 128),
            buf(F32, 2, WIDE),
            buf(BF16, 2, WIDE, 128),
            buf(BF16, 2, 128, WIDE),
            buf(F32, 16, PATCH), buf(F32, 16, PATCH), buf(F32, 2, 8, PATCH), buf(F32, 3, 2, 8, PATCH),
            buf(F32, 16, PATCH), buf(F32, 16, PATCH), buf(F32, 2, 8, PATCH), buf(F32, 3, 2, 8, PATCH),
            buf(BF16, 2, 16, 16, HID),
            buf(BF16, 16, 16, HID),
            buf(BF16, 16, 16, HID),
            buf(BF16, 16, 16, HID),
            buf(BF16, 16, HID),
            buf(BF16, 8, 16, HID),
            buf(BF16, 2, 16, 16, HID),
            buf(F32, 8, 128),
            buf(F32, 16, 8, 128),
            buf(F32, 8, 128),
            buf(F32, 8, 8, 128),
            buf(F32, 8, 128),
            buf(F32, 8, 128),
            dma((4,)), dma((7,)), dma, dma, dma((7,)), dma, dma,
            dma, dma, dma((16,)), dma, dma((8,)), dma, dma((16,)), dma((16,)), dma((16,)), dma,
            dma((16,)), dma, dma((8,)), dma, dma, dma,
        ],
        compiler_params=pltpu.CompilerParams(
            collective_id=0, has_side_effects=True, vmem_limit_bytes=48 * 1024 * 1024
        ),
    )(
        patches, cotangent, w_in, w_out,
        b_in.reshape(1, HID), gain.reshape(IMG, LOCAL), bias.reshape(IMG, LOCAL),
    )
    return out, dwin, dwout, db.reshape(HID), norm[0], norm[1]


def solution(mesh):
    placed = (P("dp", None, "chan"), P("dp", None, "chan"), P(), P(), P(), P(), P())
    return jax.shard_map(
        shards,
        mesh=mesh,
        in_specs=placed,
        out_specs=(P("dp", None, "chan"), P(), P(), P(), P("chan"), P("chan")),
        check_vma=False,
    )
```

time: 306 us -> 56.5 us (0.18)
  waiting for transfers between devices: 222 us -> 0 us
  Pallas kernels: 0 us -> 44.3 us
  blocking collectives: 30.8 us -> 0 us
  starting transfers between devices: 17.5 us -> 0 us
  between operations: 14.2 us -> 0.69 us
  other arithmetic: 7.67 us -> 0.61 us
  matrix products: 5.99 us -> 0 us
  local copies, waits for them, and re-layouts: 7.04 us -> 10.6 us
    psum x1 -> x0, waiting for transfers between devices: 216 us -> none  [together_2(): so_far = lax.psum(flat, axis)]
    pallas_call x0 -> x1, Pallas kernels: none -> 44.3 us  [shards(): pl.pallas_call(kernel, out_shape=(jax.ShapeDtypeStruct((IMG, PATCH, LOCAL...]
    all_gather x2 -> x0, blocking collectives: 30.8 us -> none  [total_of_pieces(): return lax.all_gather(shard, axis).sum(0)]
    all_to_all x2 -> x0, starting transfers between devices: 17.4 us -> none  [from_everyone(): return lax.all_to_all(copies, axis, split_axis=0, concat_axis=0, tiled=True)]
    unnamed x15 -> x21, local copies, waits for them, and re-layouts: 1.86 us -> 8.47 us
    all_to_all x2 -> x0, waiting for transfers between devices: 6.49 us -> none  [from_everyone(): return lax.all_to_all(copies, axis, split_axis=0, concat_axis=0, tiled=True)]
    dot_general x5 -> x0, matrix products: 5.99 us -> none  [the longest x1 1.84 us: shards(): jnp.einsum('pk,bpc->bkc', w_token_out, cotangent, preferred_element_type=...]
    div x6 -> x0, other arithmetic: 3.3 us -> none  [the longest x1 1.37 us: shards(): summed[1] / images]
  transfers between devices with their start and end apart: 3 -> 0, of which waited for: 2 -> 0; matrix products, arithmetic and copies ran while one was open for 1% -> 0% of each run, Pallas kernels for 0% -> 0%
where the time goes in v2:
time: 56.5 us; the launch traced here: 56.2 us
  Pallas kernels  44.3 us (78%)
  local copies, waits for them, and re-layouts  10.6 us (19%)
  between operations  0.69 us (1%)
  other arithmetic  0.61 us (1%)
    pallas_call x1, Pallas kernels, shards(): pl.pallas_call(kernel, out_shape=(jax.ShapeDtypeStruct((IMG, PATCH, LOCAL...  44.3 us
    unnamed x21, local copies, waits for them, and re-layouts  8.47 us

profile of v2, /device:TPU:1, one launch (start us, length us, event | category | flops | bytes accessed | tf_op | source)
XLA Modules:
  0.0 56.2 jit_solution(1599316379882717518)
XLA Ops:
  0.6 0.7 %reshape.24.b_ref = f32[1,640]{1,0:T(1,128)S(1)} reshape(f32[640]{0:T(1024)} %param.10) | data formatting | bytes 5120 | tf_op jit(solution)/shard_map/reshape | solution.py:345
  1.3 0.0 copy-start.7
  1.3 0.8 %reshape.25.gain_ref = f32[8,160]{1,0:T(8,128)S(1)} reshape(f32[1280]{0:T(1024)} %param.12) | data formatting | bytes 10240 | tf_op jit(solution)/shard_map/reshape | solution.py:345
  2.1 0.0 copy-done.7
  2.1 0.1 reshape.26.bias_ref
  2.2 0.0 copy-start.6
  2.2 1.5 %copy.13.x_hbm = bf16[8,256,160]{2,1,0:T(8,128)(2,1)S(1)} copy(bf16[8,256,160]{1,2,0:T(8,128)(2,1)} %param.7) | data formatting | bytes 1310720 | tf_op args[0]
  3.7 0.0 copy-done.6
  3.7 0.0 copy-start.4
  3.7 0.5 copy.14.g_hbm
  4.2 0.5 copy-done.4
  4.7 0.0 copy-start.5
  4.7 1.0 %copy-done.5 = bf16[256,640]{1,0:T(8,128)(2,1)S(1)} copy-done((bf16[256,640]{1,0:T(8,128)(2,1)S(1)}, bf16[256,640]{1,0:T(8,128)(2,1)}, u32[]{:S(2)}) %copy-start.5) | copy-done | bytes 327704
  5.6 44.3 %shard_map.118 = (bf16[8,256,160]{2,1,0:T(8,128)(2,1)S(1)}, f32[640,256]{1,0:T(8,128)S(1)}, f32[256,640]{1,0:T(8,128)S(1)}, f32[1,640]{1,0:T(1,128)S(1)}, f32[2,160]{1,0:T(2,128)S(1)}) custom-call(bf16[8,256,160]{2,1,0:T(8,128)(2,1)S(1)} %copy.13.x_hbm, bf16[8,256,160]{2,1,0:T(8,128)(2,1)S(1)} %copy.14.g_hbm, bf16[640,256]{1,0:T(8,128)(2,1)S(1)} %copy-done.4, ...), custom_call_target="tpu_custom_call" | custom-call | tf_op jit(solution)/shard_map/pallas_call | solution.py:292
  50.0 0.0 copy-start
  50.0 0.8 %copy-done = f32[256,640]{1,0:T(8,128)} copy-done((f32[256,640]{1,0:T(8,128)}, f32[256,640]{1,0:T(8,128)S(1)}, u32[]{:S(2)}) %copy-start) | copy-done | bytes 655384
  50.8 0.0 copy-start.2
  50.8 0.8 %copy-done.2 = f32[640,256]{1,0:T(8,128)} copy-done((f32[640,256]{1,0:T(8,128)}, f32[640,256]{1,0:T(8,128)S(1)}, u32[]{:S(2)}) %copy-start.2) | copy-done | bytes 655384
  51.7 0.0 copy-start.3
  51.7 1.2 %copy.15 = bf16[8,256,160]{1,2,0:T(8,128)(2,1)} copy(bf16[8,256,160]{2,1,0:T(8,128)(2,1)S(1)} %get-tuple-element.16) | data formatting | bytes 1310720
  52.9 0.6 %fusion = (f32[1,160]{1,0:T(1,128)}, f32[1,160]{1,0:T(1,128)}) fusion(f32[2,160]{1,0:T(2,128)S(1)} %get-tuple-element.15), kind=kLoop, calls=%fused_computation | loop fusion | bytes 2560 | tf_op jit(solution)/shard_map/slice | solution.py:347
  53.5 0.6 %reduce = f32[640]{0:T(1024)} reduce(f32[1,640]{1,0:T(1,128)S(1)} %get-tuple-element.14, f32[]{:T(128)} %constant.2), dimensions={0}, to_apply=%get-tuple-element.14.reduce_sub_computation | reduce | bytes 5124 | tf_op jit(solution)/shard_map/pallas_call | solution.py:292
  54.1 0.0 copy-done.3
  54.1 0.0 copy-start.1
  54.1 0.8 %copy.18 = f32[640,256]{1,0:T(8,128)} copy(f32[640,256]{1,0:T(8,128)S(1)} %copy-done.3) | data formatting | bytes 1310720
  54.9 0.5 copy-done.1
  55.4 0.8 %copy.19 = f32[256,640]{1,0:T(8,128)} copy(f32[256,640]{1,0:T(8,128)S(1)} %copy-done.1) | data formatting | bytes 1310720
Async XLA Ops:
  1.3 0.8 %copy-start.7 = (f32[1280]{0:T(1024)S(1)}, f32[1280]{0:T(1024)}, u32[]{:S(2)}) copy-start(f32[1280]{0:T(1024)} %param.13) | copy-start | bytes 15364
  2.2 1.5 %copy-start.6 = (bf16[8,256,160]{1,2,0:T(8,128)(2,1)S(1)}, bf16[8,256,160]{1,2,0:T(8,128)(2,1)}, u32[]{:S(2)}) copy-start(bf16[8,256,160]{1,2,0:T(8,128)(2,1)} %param.8) | copy-start | bytes 1966084
  3.7 1.0 %copy-start.4 = (bf16[640,256]{1,0:T(8,128)(2,1)S(1)}, bf16[640,256]{1,0:T(8,128)(2,1)}, u32[]{:S(2)}) copy-start(bf16[640,256]{1,0:T(8,128)(2,1)} %win_hbm.1) | copy-start | bytes 983044
  4.7 1.0 %copy-start.5 = (bf16[256,640]{1,0:T(8,128)(2,1)S(1)}, bf16[256,640]{1,0:T(8,128)(2,1)}, u32[]{:S(2)}) copy-start(bf16[256,640]{1,0:T(8,128)(2,1)} %wout_hbm.1) | copy-start | bytes 983044
  50.0 0.8 %copy-start = (f32[256,640]{1,0:T(8,128)}, f32[256,640]{1,0:T(8,128)S(1)}, u32[]{:S(2)}) copy-start(f32[256,640]{1,0:T(8,128)S(1)} %get-tuple-element.32) | copy-start | bytes 1966084
  50.8 0.8 %copy-start.2 = (f32[640,256]{1,0:T(8,128)}, f32[640,256]{1,0:T(8,128)S(1)}, u32[]{:S(2)}) copy-start(f32[640,256]{1,0:T(8,128)S(1)} %get-tuple-element.31) | copy-start | bytes 1966084
  51.7 2.4 %copy-start.3 = (f32[640,256]{1,0:T(8,128)S(1)}, f32[640,256]{1,0:T(8,128)}, u32[]{:S(2)}) copy-start(f32[640,256]{1,0:T(8,128)} %copy-done.2) | copy-start | bytes 1966084
  54.1 1.3 %copy-start.1 = (f32[256,640]{1,0:T(8,128)S(1)}, f32[256,640]{1,0:T(8,128)}, u32[]{:S(2)}) copy-start(f32[256,640]{1,0:T(8,128)} %copy-done) | copy-start | bytes 1966084

commit v3 on v2

v3 whole, which is shorter than its diff:
```python
import math

import jax
import jax.numpy as jnp
from jax import lax
from jax.experimental import pallas as pl
from jax.experimental.pallas import tpu as pltpu
from jax.sharding import PartitionSpec as P

CHANNELS = 1280
PATCH = 256
HID = 640
LOCAL = 160
IMG = 8
ROWS = IMG * LOCAL
IMAGES = 256
MESH = pl.DeviceIdType.MESH
eps_norm = 1e-05
F32, BF16 = jnp.float32, jnp.bfloat16


def remote(src, dst, send, recv, dev):
    return pltpu.make_async_remote_copy(
        src_ref=src, dst_ref=dst, send_sem=send, recv_sem=recv, device_id=dev, device_id_type=MESH
    )


def arrived(ref, sem):
    pltpu.make_async_copy(ref, ref, sem).wait()


def place():
    dp, ch = lax.axis_index("dp"), lax.axis_index("chan")
    x, zl, y = dp // 8, (dp // 4) % 2, dp % 4
    zh, core = ch // 2, ch % 2
    return x, y, zh * 2 + zl, core


def device(x, y, z, core):
    return (x * 8 + (z % 2) * 4 + y, (z // 2) * 2 + core)


def dot(a, b):
    return jnp.dot(a, b, preferred_element_type=F32)


def dot_nt(a, b):
    return lax.dot_general(a, b, (((1,), (1,)), ((), ())), preferred_element_type=F32)


def slot(which, image):
    return image // 4 * 8 + which * 4 + image % 4


def kernel(
    x_hbm, g_hbm, win_hbm, wout_hbm, b_hbm, gain_hbm, bias_hbm,
    out_ref, full, sum_ref,
    xv, win, wout, winT, bv, gv, rows10, left, flip, right, ga, xh, rs, gn, gcol,
    e_src, e_in, e_sum, e_far, f_src, f_in, f_sum, f_far,
    grads, r0, s, r1, t, r2, small, sm1, smt, sm2, sm3, sm4,
    ld, es, eq1, eq2, fs, fq1, fq2, s0, q0, s1, q1, s2, q2, s3, q3, s4, q4, a1, b1, a2, b2, a3, b3,
):
    x, y, z, core = place()
    other = 1 - core
    q = x * 4 + y
    partner = device(x, y, z, other)
    sends = []

    def start(c):
        c.start()
        sends.append(c)

    def plane(j):
        xx, yy = (x + j // 4) % 4, (y + j % 4) % 4
        return device(xx, yy, z, core), xx * 4 + yy

    def column(d, c=core):
        return device(x, y, (z + d) % 8, c)

    def image(b):
        return pl.ds(b * LOCAL, LOCAL)

    loads = [
        pltpu.make_async_copy(a, b, ld.at[i])
        for i, (a, b) in enumerate(
            (
                (x_hbm, xv), (g_hbm, left.at[1]), (wout_hbm, wout), (win_hbm, win),
                (b_hbm, bv), (gain_hbm, gv.at[0]), (bias_hbm, gv.at[1]),
            )
        )
    ]
    for c in loads:
        c.start()

    barrier = pltpu.get_barrier_semaphore()
    peers = [partner] + [plane(j)[0] for j in range(1, 16)] + [column(d) for d in range(1, 8)]
    peers += [column(d, other) for d in (2, 4, 6)]
    for dev in peers:
        pl.semaphore_signal(barrier, inc=1, device_id=dev, device_id_type=MESH)

    loads[0].wait()
    for b in range(IMG):
        v = xv[image(b), :].astype(F32)
        e_src[pl.ds(slot(0, b), 1), :] = jnp.sum(v, axis=0, keepdims=True)
        e_src[pl.ds(slot(1, b), 1), :] = jnp.sum(v * v, axis=0, keepdims=True)
    pl.semaphore_wait(barrier, len(peers))
    start(remote(e_src, e_in, es.at[0], eq1, partner))

    def second_step(src, came, summed, far, sem1, send, sem2):
        arrived(came, sem1)
        both = src[...] + came[...]
        summed[0] = both[:8]
        summed[1] = both[8:]
        n = 1
        for d in (4, 2, 6):
            for c in (core, other):
                start(remote(summed.at[core], far.at[d // 2 - 1, core], send.at[n], sem2, column(d, c)))
                n += 1

    def finish(summed, far, sem2):
        arrived(far, sem2)
        tot = (summed[...] + far[0] + far[1] + far[2]) * (1.0 / CHANNELS)
        return lambda which, b: tot[b // 4, which * 4 + b % 4 : which * 4 + b % 4 + 1, :]

    for c in loads[1:]:
        c.wait()
    where = z // 2 * 2 + core
    for i in range(2):
        rows10[...] = gv[i, 0].reshape(10, 128)
        at = where * 5 // 4
        both = jnp.concatenate([rows10[pl.ds(at, 1), :], rows10[pl.ds(at + 1, 1), :]], axis=1)
        mine = pltpu.roll(both, (256 - where * 5 % 4 * 32) % 256, 1)
        col = jnp.transpose(jnp.broadcast_to(mine, (128, 256)))
        gcol[i] = jnp.broadcast_to(col[:LOCAL, 0:1], (LOCAL, PATCH))
    second_step(e_src, e_in, e_sum, e_far, eq1, es, eq2)
    winT[...] = jnp.transpose(win[...])
    for b in range(IMG):
        ga[image(b), :] = dot(left[1, image(b), :], wout[...])
    flip[1] = jnp.transpose(left[1])

    moment = finish(e_sum, e_far, eq2)
    bias = bv[...].reshape(1, HID)
    for b in range(IMG):
        mean = moment(0, b)
        rstd = lax.rsqrt(moment(1, b) - mean * mean + eps_norm)
        rs[pl.ds(b, 1), :] = rstd
        xhat = (xv[image(b), :].astype(F32) - mean) * rstd
        xh[image(b), :] = xhat
        normed = (xhat * gcol[0] + gcol[1]).astype(BF16)
        left[0, image(b), :] = normed
        pre = dot(normed, winT[...]) + bias
        cdf = 0.5 * (1.0 + lax.erf(pre * (1.0 / math.sqrt(2.0))))
        right[1, image(b), :] = (pre * cdf).astype(BF16)
        slope = cdf + pre * jnp.exp(-0.5 * pre * pre) * (1.0 / math.sqrt(2.0 * math.pi))
        right[0, image(b), :] = (ga[image(b), :] * slope).astype(BF16)
    flip[0] = jnp.transpose(left[0])

    grads[other] = dot(flip[other], right[other]).astype(BF16).reshape(16, 16, HID)
    start(remote(grads.at[other], r0, s0, q0, partner))
    grads[core] = dot(flip[core], right[core]).astype(BF16).reshape(16, 16, HID)
    arrived(r0, q0)
    for i in range(16):
        s[i] = (grads[core, i].astype(F32) + r0[i].astype(F32)).astype(BF16)
    for j in range(1, 16):
        dev, qq = plane(j)
        start(remote(s.at[qq], r1.at[j], s1.at[j], q1, dev))

    by_gain = by_shift = None
    for b in range(IMG):
        v = dot(right[0, image(b), :], win[...]).astype(BF16)
        gn[image(b), :] = v
        v = v.astype(F32)
        along = v * xh[image(b), :]
        f_src[pl.ds(slot(0, b), 1), :] = jnp.sum(v * gcol[0], axis=0, keepdims=True)
        f_src[pl.ds(slot(1, b), 1), :] = jnp.sum(along * gcol[0], axis=0, keepdims=True)
        by_gain = along if b == 0 else by_gain + along
        by_shift = v if b == 0 else by_shift + v
    start(remote(f_src, f_in, fs.at[0], fq1, partner))

    db = dot(jnp.ones((8, ROWS), BF16), right[0])[0:1]
    for i in range(5):
        small[pl.ds(i, 1), :] = db[:, i * 128 : i * 128 + 128]
    ones = jnp.ones((8, PATCH), BF16)
    for i, v in enumerate((by_gain, by_shift)):
        hi = v.astype(BF16)
        rest = v - hi.astype(F32)
        mid = rest.astype(BF16)
        low = (rest - mid.astype(F32)).astype(BF16)
        one = (dot_nt(ones, hi) + dot_nt(ones, mid) + dot_nt(ones, low))[0:1]
        small[pl.ds(5 + i, 1), :] = one[:, :128]
        small[pl.ds(7, 1), pl.ds(32 * i, 32)] = one[:, 128:]
    small[pl.ds(7, 1), pl.ds(64, 64)] = jnp.zeros((1, 64), F32)
    for j in range(1, 16):
        start(remote(small, sm1.at[j], a1.at[j], b1, plane(j)[0]))

    second_step(f_src, f_in, f_sum, f_far, fq1, fs, fq2)

    arrived(r1.at[pl.ds(1, 15)], q1)
    acc = s[q].astype(F32)
    for j in range(1, 16):
        acc = acc + r1[j].astype(F32)
    t[...] = acc.astype(BF16)
    for d in (4, 3, 5, 2, 6, 1, 7):
        start(remote(t, r2.at[d], s2.at[d], q2, column(d)))

    moment = finish(f_sum, f_far, fq2)
    for b in range(IMG):
        inner = gn[image(b), :].astype(F32) * gcol[0] - moment(0, b) - xh[image(b), :] * moment(1, b)
        out_ref[image(b), :] = (left[1, image(b), :].astype(F32) + rs[pl.ds(b, 1), :] * inner).astype(BF16)

    arrived(r2.at[pl.ds(1, 7)], q2)
    acc = t[...].astype(F32)
    for d in range(1, 8):
        acc = acc + r2[d].astype(F32)
    full[core, q] = acc.astype(BF16)
    for j in range(1, 16):
        start(remote(full.at[core, q], full.at[core, q], s3.at[j], q3.at[j], plane(j)[0]))
    start(remote(full.at[core, q], full.at[core, q], s4.at[0], q4, partner))

    arrived(sm1.at[pl.ds(1, 15)], b1)
    acc = small[...]
    for j in range(1, 16):
        acc = acc + sm1[j]
    smt[...] = acc
    for d in range(1, 8):
        start(remote(smt, sm2.at[d], a2.at[d], b2, column(d)))

    for j in range(1, 16):
        xx, yy = (x + 4 - j // 4) % 4, (y + 4 - j % 4) % 4
        qq = xx * 4 + yy
        arrived(full.at[core, qq], q3.at[j])
        start(remote(full.at[core, qq], full.at[core, qq], s4.at[j], q4, partner))

    arrived(sm2.at[pl.ds(1, 7)], b2)
    near = smt[...] + sm2[7 - 6 * (z % 2)]
    acc = smt[...]
    for d in range(1, 8):
        acc = acc + sm2[d]
    sm3[...] = acc
    start(remote(sm3, sm4, a3, b3, partner))
    arrived(sm4, b3)
    row = lax.broadcasted_iota(jnp.int32, (8, 128), 0)
    sum_ref[...] = jnp.where(row < 5, sm3[...] + sm4[...], near) * (1.0 / IMAGES)
    arrived(full.at[other], q4)
    for c in sends:
        c.wait_send()


def last_kernel(d_ref, full, sum_ref, out, dwin, dwout, db, gain, shift, v1, v2, v3, v4, v5, sem):
    copies = []

    def put(i, src, dst):
        c = pltpu.make_async_copy(src, dst, sem.at[i])
        c.start()
        copies.append(c)

    put(0, d_ref, out)
    v2[...] = full[1].reshape(PATCH, HID).astype(F32) * (1.0 / IMAGES)
    put(1, v2, dwout)
    v1[...] = jnp.transpose(full[0].reshape(PATCH, HID).astype(F32)) * (1.0 / IMAGES)
    put(2, v1, dwin)
    v3[...] = sum_ref[0:5, :].reshape(HID)
    put(3, v3, db)
    for i, (v, dst) in enumerate(((v4, gain), (v5, shift))):
        v[pl.ds(0, 128)] = sum_ref[5 + i, :]
        v[pl.ds(128, 32)] = sum_ref[7, 32 * i : 32 * i + 32]
        put(4 + i, v, dst)
    for c in copies:
        c.wait()


def buf(dtype, *shape):
    return pltpu.VMEM(shape, dtype)


def shards(patches, cotangent, w_in, b_in, w_out, gain, bias):
    dma = pltpu.SemaphoreType.DMA
    vmem = pl.BlockSpec(memory_space=pltpu.VMEM)
    hbm = pl.BlockSpec(memory_space=pltpu.HBM)

    def turned(v):
        return v.transpose(0, 2, 1).reshape(ROWS, PATCH)

    d, full, sums = pl.pallas_call(
        kernel,
        out_shape=(
            jax.ShapeDtypeStruct((ROWS, PATCH), BF16),
            jax.ShapeDtypeStruct((2, 16, 16, HID), BF16),
            jax.ShapeDtypeStruct((8, 128), F32),
        ),
        in_specs=[hbm] * 7,
        out_specs=(vmem,) * 3,
        scratch_shapes=[
            buf(BF16, ROWS, PATCH),
            buf(BF16, HID, PATCH),
            buf(BF16, PATCH, HID),
            buf(BF16, PATCH, HID),
            buf(F32, 1, HID),
            buf(F32, 2, 1, CHANNELS),
            buf(F32, 10, 128),
            buf(BF16, 2, ROWS, PATCH),
            buf(BF16, 2, PATCH, ROWS),
            buf(BF16, 2, ROWS, HID),
            buf(F32, ROWS, HID),
            buf(F32, ROWS, PATCH),
            buf(F32, 8, PATCH),
            buf(BF16, ROWS, PATCH),
            buf(F32, 2, LOCAL, PATCH),
            buf(F32, 16, PATCH), buf(F32, 16, PATCH), buf(F32, 2, 8, PATCH), buf(F32, 3, 2, 8, PATCH),
            buf(F32, 16, PATCH), buf(F32, 16, PATCH), buf(F32, 2, 8, PATCH), buf(F32, 3, 2, 8, PATCH),
            buf(BF16, 2, 16, 16, HID),
            buf(BF16, 16, 16, HID),
            buf(BF16, 16, 16, HID),
            buf(BF16, 16, 16, HID),
            buf(BF16, 16, HID),
            buf(BF16, 8, 16, HID),
            buf(F32, 8, 128),
            buf(F32, 16, 8, 128), buf(F32, 8, 128), buf(F32, 8, 8, 128), buf(F32, 8, 128), buf(F32, 8, 128),
            dma((7,)), dma((7,)), dma, dma, dma((7,)), dma, dma,
            dma, dma, dma((16,)), dma, dma((8,)), dma, dma((16,)), dma((16,)), dma((16,)), dma,
            dma((16,)), dma, dma((8,)), dma, dma, dma,
        ],
        compiler_params=pltpu.CompilerParams(collective_id=0, has_side_effects=True),
    )(
        turned(patches), turned(cotangent), w_in, w_out,
        b_in.reshape(1, HID), gain.reshape(1, CHANNELS), bias.reshape(1, CHANNELS),
    )
    out, dwin, dwout, db, dgain, dshift = pl.pallas_call(
        last_kernel,
        out_shape=(
            jax.ShapeDtypeStruct((ROWS, PATCH), BF16),
            jax.ShapeDtypeStruct((HID, PATCH), F32),
            jax.ShapeDtypeStruct((PATCH, HID), F32),
            jax.ShapeDtypeStruct((HID,), F32),
            jax.ShapeDtypeStruct((LOCAL,), F32),
            jax.ShapeDtypeStruct((LOCAL,), F32),
        ),
        in_specs=[vmem] * 3,
        out_specs=(hbm,) * 6,
        scratch_shapes=[
            buf(F32, HID, PATCH), buf(F32, PATCH, HID), buf(F32, HID), buf(F32, LOCAL), buf(F32, LOCAL), dma((6,)),
        ],
    )(d, full, sums)
    return out.reshape(IMG, LOCAL, PATCH).transpose(0, 2, 1), dwin, dwout, db, dgain, dshift


def solution(mesh):
    placed = (P("dp", None, "chan"), P("dp", None, "chan"), P(), P(), P(), P(), P())
    return jax.shard_map(
        shards,
        mesh=mesh,
        in_specs=placed,
        out_specs=(P("dp", None, "chan"), P(), P(), P(), P("chan"), P("chan")),
        check_vma=False,
    )
```

time: 56.5 us -> 49.9 us (0.88)
  local copies, waits for them, and re-layouts: 10.6 us -> 2.57 us
  Pallas kernels: 44.3 us -> 46.4 us
  other arithmetic: 0.61 us -> 0 us
    unnamed x21 -> x4, local copies, waits for them, and re-layouts: 8.47 us -> 0.11 us
    pallas_call x1 -> x2, Pallas kernels: 44.3 us -> 46.4 us  [the longest x1 43.8 us: shards(): pl.pallas_call(kernel, out_shape=(jax.ShapeDtypeStruct((ROWS, PATCH), BF1...]
    pallas_call x1 -> x0, other arithmetic: 0.61 us -> none  [shards(): pl.pallas_call(kernel, out_shape=(jax.ShapeDtypeStruct((IMG, PATCH, LOCAL...]
    reshape x1, local copies, waits for them, and re-layouts: 0.69 us -> 1.27 us  [shards(): b_in.reshape(1, HID)]
    slice x1 -> x0, local copies, waits for them, and re-layouts: 0.57 us -> none  [shards(): return (out, dwin, dwout, db.reshape(HID), norm[0], norm[1])]
where the time goes in v3:
time: 49.9 us; the launch traced here: 49.7 us
  Pallas kernels  46.4 us (93%)
  local copies, waits for them, and re-layouts  2.57 us (5%)
  between operations  0.65 us (1%)
    pallas_call x1, Pallas kernels, shards(): pl.pallas_call(kernel, out_shape=(jax.ShapeDtypeStruct((ROWS, PATCH), BF1...  43.8 us
    pallas_call x1, Pallas kernels, shards(): pl.pallas_call(last_kernel, out_shape=(jax.ShapeDtypeStruct((ROWS, PATCH)...  2.61 us
    reshape x1, local copies, waits for them, and re-layouts, shards(): b_in.reshape(1, HID)  1.27 us

profile of v3, /device:TPU:1, one launch (start us, length us, event | category | flops | bytes accessed | tf_op | source)
XLA Modules:
  0.0 49.7 jit_solution(5610557406448950506)
XLA Ops:
  0.6 0.0 copy-start
  0.6 1.3 %reshape.32.b_hbm = f32[1,640]{1,0:T(1,128)} reshape(f32[640]{0:T(1024)} %param.10) | data formatting | bytes 5120 | tf_op jit(solution)/shard_map/reshape | solution.py:326
  1.9 0.0 copy-done
  1.9 0.0 copy-start.1
  1.9 0.6 %reshape.33.gain_hbm = f32[1,1280]{1,0:T(1,128)} reshape(f32[1280]{0:T(1024)S(1)} %copy-done) | data formatting | bytes 10240 | tf_op jit(solution)/shard_map/reshape | solution.py:326
  2.5 0.1 copy-done.1
  2.6 0.6 %reshape.34.bias_hbm = f32[1,1280]{1,0:T(1,128)} reshape(f32[1280]{0:T(1024)S(1)} %copy-done.1) | data formatting | bytes 10240 | tf_op jit(solution)/shard_map/reshape | solution.py:326
  3.2 43.8 %shard_map.118 = (bf16[1280,256]{1,0:T(8,128)(2,1)}, bf16[2,16,16,640]{3,2,1,0:T(8,128)(2,1)}, f32[8,128]{1,0:T(8,128)}) custom-call(bf16[1280,256]{1,0:T(8,128)(2,1)} %bitcast.9, bf16[1280,256]{1,0:T(8,128)(2,1)} %bitcast.10, bf16[640,256]{1,0:T(8,128)(2,1)} %win_hbm.1, bf16[256,640]{1,0:T(8,128)(2,1)} %wout_hbm.1, f32[1,640]{1,0:T(1,128)} %reshape.32.b_hbm, ...), custom_call_target="tpu_custom_call" | custom-call | tf_op jit(solution)/shard_map/pallas_call | solution.py:284
  47.0 2.6 %shard_map.119 = (bf16[1280,256]{1,0:T(8,128)(2,1)}, f32[640,256]{1,0:T(8,128)}, f32[256,640]{1,0:T(8,128)}, f32[640]{0:T(1024)}, f32[160]{0:T(256)}, /*index=5*/f32[160]{0:T(256)}) custom-call(bf16[1280,256]{1,0:T(8,128)(2,1)} %get-tuple-element.15.d_ref, bf16[2,16,16,640]{3,2,1,0:T(8,128)(2,1)} %get-tuple-element.16.full, f32[8,128]{1,0:T(8,128)} %get-tuple-element.17.sum_ref), custom_call_target="tpu_custom_call" | custom-call | tf_op jit(solution)/shard_map/pallas_call | solution.py:328
Async XLA Ops:
  0.6 1.3 %copy-start = (f32[1280]{0:T(1024)S(1)}, f32[1280]{0:T(1024)}, u32[]{:S(2)}) copy-start(f32[1280]{0:T(1024)} %param.12) | copy-start | bytes 15364
  1.9 0.7 %copy-start.1 = (f32[1280]{0:T(1024)S(1)}, f32[1280]{0:T(1024)}, u32[]{:S(2)}) copy-start(f32[1280]{0:T(1024)} %param.13) | copy-start | bytes 15364

commit v4 on v3

--- a/solution.py
+++ b/solution.py
@@ -15,6 +15,9 @@
 ROWS = IMG * LOCAL
 IMAGES = 256
 MESH = pl.DeviceIdType.MESH
+PIECES = ((0, 384), (384, 256))
+FAR_FIRST = sorted(range(1, 16), key=lambda j: -min(j // 4, 4 - j // 4) - min(j % 4, 4 - j % 4))
+Z_FAR_FIRST = (4, 3, 5, 2, 6, 1, 7)
 eps_norm = 1e-05
 F32, BF16 = jnp.float32, jnp.bfloat16
 
@@ -54,17 +57,19 @@
 
 def kernel(
     x_hbm, g_hbm, win_hbm, wout_hbm, b_hbm, gain_hbm, bias_hbm,
-    out_ref, full, sum_ref,
-    xv, win, wout, winT, bv, gv, rows10, left, flip, right, ga, xh, rs, gn, gcol,
+    out_ref, full_a, full_b, sum_ref,
+    xv, win, wout, winT, bv, gain_v, bias_v, rows5, rows10, left, flip, right, ga, xh, rs, gn, gcol,
     e_src, e_in, e_sum, e_far, f_src, f_in, f_sum, f_far,
-    grads, r0, s, r1, t, r2, small, sm1, smt, sm2, sm3, sm4,
-    ld, es, eq1, eq2, fs, fq1, fq2, s0, q0, s1, q1, s2, q2, s3, q3, s4, q4, a1, b1, a2, b2, a3, b3,
+    small, sm1, smt, sm2, sm3, sm4,
+    ld, es, eq1, eq2, fs, fq1, fq2, a1, b1, a2, b2, a3, b3, *travel,
 ):
     x, y, z, core = place()
     other = 1 - core
     q = x * 4 + y
     partner = device(x, y, z, other)
     sends = []
+    fulls = (full_a, full_b)
+    travel = (travel[:16], travel[16:])
 
     def start(c):
         c.start()
@@ -84,12 +89,15 @@
         pltpu.make_async_copy(a, b, ld.at[i])
         for i, (a, b) in enumerate(
             (
-                (x_hbm, xv), (g_hbm, left.at[1]), (wout_hbm, wout), (win_hbm, win),
-                (b_hbm, bv), (gain_hbm, gv.at[0]), (bias_hbm, gv.at[1]),
+                (g_hbm, left.at[1]), (wout_hbm, wout), (win_hbm, win),
+                (b_hbm, bv), (gain_hbm, gain_v), (bias_hbm, bias_v),
             )
         )
     ]
-    for c in loads:
+    x_loads = [
+        pltpu.make_async_copy(x_hbm.at[image(b)], xv.at[image(b)], ld.at[8 + b]) for b in range(IMG)
+    ]
+    for c in x_loads + loads:
         c.start()
 
     barrier = pltpu.get_barrier_semaphore()
@@ -98,8 +106,8 @@
     for dev in peers:
         pl.semaphore_signal(barrier, inc=1, device_id=dev, device_id_type=MESH)
 
-    loads[0].wait()
-    for b in range(IMG):
+    for b in range(IMG):
+        x_loads[b].wait()
         v = xv[image(b), :].astype(F32)
         e_src[pl.ds(slot(0, b), 1), :] = jnp.sum(v, axis=0, keepdims=True)
         e_src[pl.ds(slot(1, b), 1), :] = jnp.sum(v * v, axis=0, keepdims=True)
@@ -122,24 +130,25 @@
         tot = (summed[...] + far[0] + far[1] + far[2]) * (1.0 / CHANNELS)
         return lambda which, b: tot[b // 4, which * 4 + b % 4 : which * 4 + b % 4 + 1, :]
 
-    for c in loads[1:]:
+    second_step(e_src, e_in, e_sum, e_far, eq1, es, eq2)
+    for c in loads:
         c.wait()
     where = z // 2 * 2 + core
     for i in range(2):
-        rows10[...] = gv[i, 0].reshape(10, 128)
+        rows10[...] = (gain_v, bias_v)[i][...].reshape(10, 128)
         at = where * 5 // 4
         both = jnp.concatenate([rows10[pl.ds(at, 1), :], rows10[pl.ds(at + 1, 1), :]], axis=1)
         mine = pltpu.roll(both, (256 - where * 5 % 4 * 32) % 256, 1)
         col = jnp.transpose(jnp.broadcast_to(mine, (128, 256)))
         gcol[i] = jnp.broadcast_to(col[:LOCAL, 0:1], (LOCAL, PATCH))
-    second_step(e_src, e_in, e_sum, e_far, eq1, es, eq2)
     winT[...] = jnp.transpose(win[...])
     for b in range(IMG):
         ga[image(b), :] = dot(left[1, image(b), :], wout[...])
     flip[1] = jnp.transpose(left[1])
 
     moment = finish(e_sum, e_far, eq2)
-    bias = bv[...].reshape(1, HID)
+    rows5[...] = bv[...].reshape(5, 128)
+    bias = jnp.concatenate([rows5[i : i + 1, :] for i in range(5)], axis=1)
     for b in range(IMG):
         mean = moment(0, b)
         rstd = lax.rsqrt(moment(1, b) - mean * mean + eps_norm)
@@ -148,22 +157,26 @@
         xh[image(b), :] = xhat
         normed = (xhat * gcol[0] + gcol[1]).astype(BF16)
         left[0, image(b), :] = normed
-        pre = dot(normed, winT[...]) + bias
-        cdf = 0.5 * (1.0 + lax.erf(pre * (1.0 / math.sqrt(2.0))))
-        right[1, image(b), :] = (pre * cdf).astype(BF16)
-        slope = cdf + pre * jnp.exp(-0.5 * pre * pre) * (1.0 / math.sqrt(2.0 * math.pi))
-        right[0, image(b), :] = (ga[image(b), :] * slope).astype(BF16)
     flip[0] = jnp.transpose(left[0])
 
-    grads[other] = dot(flip[other], right[other]).astype(BF16).reshape(16, 16, HID)
-    start(remote(grads.at[other], r0, s0, q0, partner))
-    grads[core] = dot(flip[core], right[core]).astype(BF16).reshape(16, 16, HID)
-    arrived(r0, q0)
-    for i in range(16):
-        s[i] = (grads[core, i].astype(F32) + r0[i].astype(F32)).astype(BF16)
-    for j in range(1, 16):
-        dev, qq = plane(j)
-        start(remote(s.at[qq], r1.at[j], s1.at[j], q1, dev))
+    for (at, width), (grads, r0, *_), sem in zip(PIECES, travel, travel):
+        ks = pl.ds(at, width)
+        for b in range(IMG):
+            pre = dot(left[0, image(b), :], winT[:, ks]) + bias[:, at : at + width]
+            cdf = 0.5 * (1.0 + lax.erf(pre * (1.0 / math.sqrt(2.0))))
+            right[1, image(b), ks] = (pre * cdf).astype(BF16)
+            slope = cdf + pre * jnp.exp(-0.5 * pre * pre) * (1.0 / math.sqrt(2.0 * math.pi))
+            right[0, image(b), ks] = (ga[image(b), ks] * slope).astype(BF16)
+        grads[other] = dot(flip[other], right[other, :, ks]).astype(BF16).reshape(16, 16, width)
+        start(remote(grads.at[other], r0, sem[6], sem[7], partner))
+        grads[core] = dot(flip[core], right[core, :, ks]).astype(BF16).reshape(16, 16, width)
+    for grads, r0, s, r1, t, r2, s0, q0, s1, q1, *_ in travel:
+        arrived(r0, q0)
+        for i in range(16):
+            s[i] = (grads[core, i].astype(F32) + r0[i].astype(F32)).astype(BF16)
+        for j in FAR_FIRST:
+            dev, qq = plane(j)
+            start(remote(s.at[qq], r1.at[j], s1.at[j], q1, dev))
 
     by_gain = by_shift = None
     for b in range(IMG):
@@ -195,41 +208,37 @@
 
     second_step(f_src, f_in, f_sum, f_far, fq1, fs, fq2)
 
-    arrived(r1.at[pl.ds(1, 15)], q1)
-    acc = s[q].astype(F32)
-    for j in range(1, 16):
-        acc = acc + r1[j].astype(F32)
-    t[...] = acc.astype(BF16)
-    for d in (4, 3, 5, 2, 6, 1, 7):
-        start(remote(t, r2.at[d], s2.at[d], q2, column(d)))
+    for grads, r0, s, r1, t, r2, s0, q0, s1, q1, s2, q2, *_ in travel:
+        arrived(r1.at[pl.ds(1, 15)], q1)
+        acc = s[q].astype(F32)
+        for j in range(1, 16):
+            acc = acc + r1[j].astype(F32)
+        t[...] = acc.astype(BF16)
+        for d in Z_FAR_FIRST:
+            start(remote(t, r2.at[d], s2.at[d], q2, column(d)))
 
     moment = finish(f_sum, f_far, fq2)
     for b in range(IMG):
         inner = gn[image(b), :].astype(F32) * gcol[0] - moment(0, b) - xh[image(b), :] * moment(1, b)
         out_ref[image(b), :] = (left[1, image(b), :].astype(F32) + rs[pl.ds(b, 1), :] * inner).astype(BF16)
-
-    arrived(r2.at[pl.ds(1, 7)], q2)
-    acc = t[...].astype(F32)
-    for d in range(1, 8):
-        acc = acc + r2[d].astype(F32)
-    full[core, q] = acc.astype(BF16)
-    for j in range(1, 16):
-        start(remote(full.at[core, q], full.at[core, q], s3.at[j], q3.at[j], plane(j)[0]))
-    start(remote(full.at[core, q], full.at[core, q], s4.at[0], q4, partner))
 
     arrived(sm1.at[pl.ds(1, 15)], b1)
     acc = small[...]
     for j in range(1, 16):
         acc = acc + sm1[j]
     smt[...] = acc
-    for d in range(1, 8):
+    for d in Z_FAR_FIRST:
         start(remote(smt, sm2.at[d], a2.at[d], b2, column(d)))
 
-    for j in range(1, 16):
-        xx, yy = (x + 4 - j // 4) % 4, (y + 4 - j % 4) % 4
-        qq = xx * 4 + yy
-        arrived(full.at[core, qq], q3.at[j])
-        start(remote(full.at[core, qq], full.at[core, qq], s4.at[j], q4, partner))
+    for full, (grads, r0, s, r1, t, r2, s0, q0, s1, q1, s2, q2, s3, q3, s4, q4) in zip(fulls, travel):
+        arrived(r2.at[pl.ds(1, 7)], q2)
+        acc = t[...].astype(F32)
+        for d in range(1, 8):
+            acc = acc + r2[d].astype(F32)
+        full[core, q] = acc.astype(BF16)
+        for j in FAR_FIRST:
+            start(remote(full.at[core, q], full.at[core, q], s3.at[j], q3.at[j], plane(j)[0]))
+        start(remote(full.at[core, q], full.at[core, q], s4.at[0], q4, partner))
 
     arrived(sm2.at[pl.ds(1, 7)], b2)
     near = smt[...] + sm2[7 - 6 * (z % 2)]
@@ -238,15 +247,22 @@
         acc = acc + sm2[d]
     sm3[...] = acc
     start(remote(sm3, sm4, a3, b3, partner))
+    for full, (*_, q3, s4, q4) in zip(fulls, travel):
+        for j in FAR_FIRST[::-1]:
+            xx, yy = (x + 4 - j // 4) % 4, (y + 4 - j % 4) % 4
+            qq = xx * 4 + yy
+            arrived(full.at[core, qq], q3.at[j])
+            start(remote(full.at[core, qq], full.at[core, qq], s4.at[j], q4, partner))
     arrived(sm4, b3)
     row = lax.broadcasted_iota(jnp.int32, (8, 128), 0)
     sum_ref[...] = jnp.where(row < 5, sm3[...] + sm4[...], near) * (1.0 / IMAGES)
-    arrived(full.at[other], q4)
+    for full, (*_, q4) in zip(fulls, travel):
+        arrived(full.at[other], q4)
     for c in sends:
         c.wait_send()
 
 
-def last_kernel(d_ref, full, sum_ref, out, dwin, dwout, db, gain, shift, v1, v2, v3, v4, v5, sem):
+def last_kernel(d_ref, full_a, full_b, sum_ref, out, dwin, dwout, db, gain, shift, v1, v2, v3, v4, v5, sem):
     copies = []
 
     def put(i, src, dst):
@@ -255,10 +271,13 @@
         copies.append(c)
 
     put(0, d_ref, out)
-    v2[...] = full[1].reshape(PATCH, HID).astype(F32) * (1.0 / IMAGES)
+    for (at, width), full in zip(PIECES, (full_a, full_b)):
+        v2[:, pl.ds(at, width)] = full[1].reshape(PATCH, width).astype(F32) * (1.0 / IMAGES)
     put(1, v2, dwout)
-    v1[...] = jnp.transpose(full[0].reshape(PATCH, HID).astype(F32)) * (1.0 / IMAGES)
-    put(2, v1, dwin)
+    for n, ((at, width), full) in enumerate(zip(PIECES, (full_a, full_b))):
+        rows = pl.ds(at, width)
+        v1[rows, :] = jnp.transpose(full[0].reshape(PATCH, width).astype(F32)) * (1.0 / IMAGES)
+        put(6 + n, v1.at[rows], dwin.at[rows])
     v3[...] = sum_ref[0:5, :].reshape(HID)
     put(3, v3, db)
     for i, (v, dst) in enumerate(((v4, gain), (v5, shift))):
@@ -281,22 +300,35 @@
     def turned(v):
         return v.transpose(0, 2, 1).reshape(ROWS, PATCH)
 
-    d, full, sums = pl.pallas_call(
+    def piece(width):
+        return [
+            buf(BF16, 2, 16, 16, width),
+            buf(BF16, 16, 16, width),
+            buf(BF16, 16, 16, width),
+            buf(BF16, 16, 16, width),
+            buf(BF16, 16, width),
+            buf(BF16, 8, 16, width),
+            dma, dma, dma((16,)), dma, dma((8,)), dma, dma((16,)), dma((16,)), dma((16,)), dma,
+        ]
+
+    d, full_a, full_b, sums = pl.pallas_call(
         kernel,
         out_shape=(
             jax.ShapeDtypeStruct((ROWS, PATCH), BF16),
-            jax.ShapeDtypeStruct((2, 16, 16, HID), BF16),
+            *(jax.ShapeDtypeStruct((2, 16, 16, width), BF16) for _, width in PIECES),
             jax.ShapeDtypeStruct((8, 128), F32),
         ),
         in_specs=[hbm] * 7,
-        out_specs=(vmem,) * 3,
+        out_specs=(vmem,) * 4,
         scratch_shapes=[
             buf(BF16, ROWS, PATCH),
             buf(BF16, HID, PATCH),
             buf(BF16, PATCH, HID),
             buf(BF16, PATCH, HID),
-            buf(F32, 1, HID),
-            buf(F32, 2, 1, CHANNELS),
+            buf(F32, HID),
+            buf(F32, CHANNELS),
+            buf(F32, CHANNELS),
+            buf(F32, 5, 128),
             buf(F32, 10, 128),
             buf(BF16, 2, ROWS, PATCH),
             buf(BF16, 2, PATCH, ROWS),
@@ -308,22 +340,18 @@
             buf(F32, 2, LOCAL, PATCH),
             buf(F32, 16, PATCH), buf(F32, 16, PATCH), buf(F32, 2, 8, PATCH), buf(F32, 3, 2, 8, PATCH),
             buf(F32, 16, PATCH), buf(F32, 16, PATCH), buf(F32, 2, 8, PATCH), buf(F32, 3, 2, 8, PATCH),
-            buf(BF16, 2, 16, 16, HID),
-            buf(BF16, 16, 16, HID),
-            buf(BF16, 16, 16, HID),
-            buf(BF16, 16, 16, HID),
-            buf(BF16, 16, HID),
-            buf(BF16, 8, 16, HID),
             buf(F32, 8, 128),
             buf(F32, 16, 8, 128), buf(F32, 8, 128), buf(F32, 8, 8, 128), buf(F32, 8, 128), buf(F32, 8, 128),
-            dma((7,)), dma((7,)), dma, dma, dma((7,)), dma, dma,
-            dma, dma, dma((16,)), dma, dma((8,)), dma, dma((16,)), dma((16,)), dma((16,)), dma,
+            dma((16,)), dma((7,)), dma, dma, dma((7,)), dma, dma,
             dma((16,)), dma, dma((8,)), dma, dma, dma,
+            *piece(PIECES[0][1]), *piece(PIECES[1][1]),
         ],
-        compiler_params=pltpu.CompilerParams(collective_id=0, has_side_effects=True),
+        compiler_params=pltpu.CompilerParams(collective_id=0, has_side_effects=True, vmem_limit_bytes=40000000),
     )(
-        turned(patches), turned(cotangent), w_in, w_out,
-        b_in.reshape(1, HID), gain.reshape(1, CHANNELS), bias.reshape(1, CHANNELS),
+        *(
+            pltpu.with_memory_space_constraint(v, pltpu.HBM)
+            for v in (turned(patches), turned(cotangent), w_in, w_out, b_in, gain, bias)
+        )
     )
     out, dwin, dwout, db, dgain, dshift = pl.pallas_call(
         last_kernel,
@@ -335,12 +363,13 @@
             jax.ShapeDtypeStruct((LOCAL,), F32),
             jax.ShapeDtypeStruct((LOCAL,), F32),
         ),
-        in_specs=[vmem] * 3,
+        in_specs=[vmem] * 4,
         out_specs=(hbm,) * 6,
         scratch_shapes=[
-            buf(F32, HID, PATCH), buf(F32, PATCH, HID), buf(F32, HID), buf(F32, LOCAL), buf(F32, LOCAL), dma((6,)),
+            buf(F32, HID, PATCH), buf(F32, PATCH, HID), buf(F32, HID), buf(F32, LOCAL), buf(F32, LOCAL), dma((8,)),
         ],
-    )(d, full, sums)
+        compiler_params=pltpu.CompilerParams(vmem_limit_bytes=8 * 1024 * 1024),
+    )(d, full_a, full_b, sums)
     return out.reshape(IMG, LOCAL, PATCH).transpose(0, 2, 1), dwin, dwout, db, dgain, dshift
 
 

time: 49.9 us -> 42.8 us (0.86)
  Pallas kernels: 46.4 us -> 42.1 us
  local copies, waits for them, and re-layouts: 2.57 us -> 0 us
    pallas_call x1, Pallas kernels: 43.8 us -> 40.7 us  [shards(): pl.pallas_call(kernel, out_shape=(jax.ShapeDtypeStruct((ROWS, PATCH), BF1...]
    reshape x3 -> x0, local copies, waits for them, and re-layouts: 2.47 us -> none  [the longest x1 1.27 us: shards(): b_in.reshape(1, HID)]
    pallas_call x1, Pallas kernels: 2.61 us -> 1.34 us  [shards(): pl.pallas_call(last_kernel, out_shape=(jax.ShapeDtypeStruct((ROWS, PATCH)...]
where the time goes in v4:
time: 42.8 us; the launch traced here: 42.7 us
  Pallas kernels  42.1 us (98%)
  between operations  0.64 us (1%)
    pallas_call x1, Pallas kernels, shards(): pl.pallas_call(kernel, out_shape=(jax.ShapeDtypeStruct((ROWS, PATCH), BF1...  40.7 us
    pallas_call x1, Pallas kernels, shards(): pl.pallas_call(last_kernel, out_shape=(jax.ShapeDtypeStruct((ROWS, PATCH)...  1.34 us

profile of v4, /device:TPU:1, one launch (start us, length us, event | category | flops | bytes accessed | tf_op | source)
XLA Modules:
  0.0 42.7 jit_solution(9505009372904396639)
XLA Ops:
  0.6 40.7 %shard_map.118 = (bf16[1280,256]{1,0:T(8,128)(2,1)S(1)}, bf16[2,16,16,384]{3,2,1,0:T(8,128)(2,1)S(1)}, bf16[2,16,16,256]{3,2,1,0:T(8,128)(2,1)S(1)}, f32[8,128]{1,0:T(8,128)S(1)}) custom-call(bf16[1280,256]{1,0:T(8,128)(2,1)} %bitcast.9, bf16[1280,256]{1,0:T(8,128)(2,1)} %bitcast.10, bf16[640,256]{1,0:T(8,128)(2,1)} %win_hbm.1, bf16[256,640]{1,0:T(8,128)(2,1)} %wout_hbm.1, ...), custom_call_target="tpu_custom_call" | custom-call | tf_op jit(solution)/shard_map/pallas_call | solution.py:314
  41.4 1.3 %shard_map.119 = (bf16[1280,256]{1,0:T(8,128)(2,1)}, f32[640,256]{1,0:T(8,128)}, f32[256,640]{1,0:T(8,128)}, f32[640]{0:T(1024)}, f32[160]{0:T(256)}, /*index=5*/f32[160]{0:T(256)}) custom-call(bf16[1280,256]{1,0:T(8,128)(2,1)S(1)} %get-tuple-element.16.d_ref, bf16[2,16,16,384]{3,2,1,0:T(8,128)(2,1)S(1)} %get-tuple-element.17.full_a, ...), custom_call_target="tpu_custom_call" | custom-call | tf_op jit(solution)/shard_map/pallas_call | solution.py:356

commit v5 on v4

v5 whole, which is shorter than its diff:
```python
import math

import jax
import jax.numpy as jnp
from jax import lax
from jax.experimental import pallas as pl
from jax.experimental.pallas import tpu as pltpu
from jax.sharding import PartitionSpec as P

CHANNELS = 1280
PATCH = 256
HID = 640
LOCAL = 160
IMG = 8
ROWS = IMG * LOCAL
IMAGES = 256
MESH = pl.DeviceIdType.MESH
PIECES = ((0, 384, False), (384, 256, True))
PARTS = {False: 16, True: 10}
eps_norm = 1e-05
F32, BF16 = jnp.float32, jnp.bfloat16


def remote(src, dst, send, recv, dev):
    return pltpu.make_async_remote_copy(
        src_ref=src, dst_ref=dst, send_sem=send, recv_sem=recv, device_id=dev, device_id_type=MESH
    )


def arrived(ref, sem):
    pltpu.make_async_copy(ref, ref, sem).wait()


def each(n, body):
    def step(i, carry):
        body(i)
        return carry

    lax.fori_loop(0, n, step, 0)


def div(a, b):
    return lax.div(jnp.int32(a), jnp.int32(b))


def rem(a, b):
    return lax.rem(jnp.int32(a), jnp.int32(b))


def place():
    dp, ch = lax.axis_index("dp"), lax.axis_index("chan")
    x, zl, y = div(dp, 8), rem(div(dp, 4), 2), rem(dp, 4)
    zh, core = div(ch, 2), rem(ch, 2)
    return x, y, zh * 2 + zl, core


def device(x, y, z, core):
    return (x * 8 + rem(z, 2) * 4 + y, div(z, 2) * 2 + core)


def dot(a, b):
    return jnp.dot(a, b, preferred_element_type=F32)


def dot_nt(a, b):
    return lax.dot_general(a, b, (((1,), (1,)), ((), ())), preferred_element_type=F32)


def slot(which, image):
    return image // 4 * 8 + which * 4 + image % 4


def kernel(
    x_hbm, g_hbm, win_hbm, wout_hbm, b_hbm, gain_hbm, bias_hbm,
    out_ref, *refs,
):
    fulls, (sum_ref, *refs) = refs[: len(PIECES)], refs[len(PIECES) :]
    travel = refs[41:]
    (
        xv, win, wout, winT, bv, gain_v, bias_v, rows5, rows10, left, flip, right, ga, xh, rs, gn, gcol,
        e_src, e_far, f_src, f_in, f_sum, f_far,
        small, sm1, smt, sm2, sm3, sm4,
        ld, es, eq, fs, fq1, fq2, a1, b1, a2, b2, a3, b3,
    ) = refs[:41]
    x, y, z, core = place()
    other = 1 - core
    q = x * 4 + y
    partner = device(x, y, z, other)
    sends = []
    pieces = []
    for (at, width, direct), full in zip(PIECES, fulls):
        n = PARTS[direct]
        pieces.append((pl.ds(at, width), direct, full, travel[:n]))
        travel = travel[n:]

    def start(c):
        c.start()
        sends.append(c)

    def plane(j, c=core):
        xx, yy = rem(x + div(j, 4), 4), rem(y + rem(j, 4), 4)
        return device(xx, yy, z, c), xx * 4 + yy

    def column(d, c=core):
        return device(x, y, rem(z + d, 8), c)

    def image(b):
        return pl.ds(b * LOCAL, LOCAL)

    loads = [
        pltpu.make_async_copy(a, b, ld.at[i])
        for i, (a, b) in enumerate(
            (
                (g_hbm, left.at[1]), (wout_hbm, wout), (win_hbm, win),
                (b_hbm, bv), (gain_hbm, gain_v), (bias_hbm, bias_v),
            )
        )
    ]
    def chan_peers():
        return [column(d, c) for d in (4, 2, 6) for c in (core, other)] + [partner]

    def hop(i):
        return 1 + rem(3 + i, 7)

    def offset(i):
        return 1 + rem(9 + i, 15)

    barrier = pltpu.get_barrier_semaphore()

    def greet(dev):
        pl.semaphore_signal(barrier, inc=1, device_id=dev, device_id_type=MESH)

    for dev in chan_peers():
        greet(dev)
    for d in (3, 5, 1, 7):
        greet(column(d))
    each(15, lambda i: greet(plane(offset(i))[0]))

    x_loads = [
        pltpu.make_async_copy(x_hbm.at[image(b)], xv.at[image(b)], ld.at[8 + b]) for b in range(IMG)
    ]
    for c in x_loads + loads:
        c.start()

    for b in range(IMG):
        x_loads[b].wait()
        v = xv[image(b), :].astype(F32)
        e_src[pl.ds(b, 1), :] = jnp.sum(v, axis=0, keepdims=True)
        e_src[pl.ds(8 + b, 1), :] = jnp.sum(v * v, axis=0, keepdims=True)
    pl.semaphore_wait(barrier, 26)
    for n, dev in enumerate(chan_peers()):
        start(remote(e_src, e_far.at[n], es.at[n], eq, dev))

    def second_step(src, came, summed, far, sem1, send, sem2):
        arrived(came, sem1)
        both = src[...] + came[...]
        summed[0] = both[:8]
        summed[1] = both[8:]
        n = 1
        for d in (4, 2, 6):
            for c in (core, other):
                start(remote(summed.at[core], far.at[d // 2 - 1, core], send.at[n], sem2, column(d, c)))
                n += 1

    def finish(summed, far, sem2):
        arrived(far, sem2)
        tot = (summed[...] + far[0] + far[1] + far[2]) * (1.0 / CHANNELS)
        return lambda which, b: tot[b // 4, which * 4 + b % 4 : which * 4 + b % 4 + 1, :]

    for c in loads:
        c.wait()
    where = div(z, 2) * 2 + core
    for i in range(2):
        rows10[...] = (gain_v, bias_v)[i][...].reshape(10, 128)
        at = div(where * 5, 4)
        both = jnp.concatenate([rows10[pl.ds(at, 1), :], rows10[pl.ds(at + 1, 1), :]], axis=1)
        mine = pltpu.roll(both, rem(256 - rem(where * 5, 4) * 32, 256), 1)
        col = jnp.transpose(jnp.broadcast_to(mine, (128, 256)))
        gcol[i] = jnp.broadcast_to(col[:LOCAL, 0:1], (LOCAL, PATCH))
    winT[...] = jnp.transpose(win[...])
    for b in range(IMG):
        ga[image(b), :] = dot(left[1, image(b), :], wout[...])
    flip[1] = jnp.transpose(left[1])

    arrived(e_far, eq)
    tot = e_src[...]
    for n in range(7):
        tot = tot + e_far[n]
    tot = tot * (1.0 / CHANNELS)
    means = tot[:8]
    rs[...] = lax.rsqrt(tot[8:] - means * means + eps_norm)
    rows5[...] = bv[...].reshape(5, 128)
    bias = jnp.concatenate([rows5[i : i + 1, :] for i in range(5)], axis=1)
    for b in range(IMG):
        xhat = (xv[image(b), :].astype(F32) - means[b : b + 1, :]) * rs[pl.ds(b, 1), :]
        xh[image(b), :] = xhat
        normed = (xhat * gcol[0] + gcol[1]).astype(BF16)
        left[0, image(b), :] = normed
    flip[0] = jnp.transpose(left[0])

    def scatter(direct, parts):
        if direct:
            grads, r1, _, _, s1, q1, *_ = parts

            def give(i):
                j = rem(10 + i, 16)
                dev, qq = plane(j, other)
                remote(grads.at[other, qq], r1.at[16 + j], s1, q1, dev).start()

            def give_own(i):
                dev, qq = plane(offset(i))
                remote(grads.at[core, qq], r1.at[offset(i)], s1, q1, dev).start()
                give(i)

            each(15, give_own)
            give(15)
            return
        grads, r0, s, r1, _, _, _, q0, s1, q1, *_ = parts
        arrived(r0, q0)

        def add(i):
            s[i] = (grads[core, i].astype(F32) + r0[i].astype(F32)).astype(BF16)

        each(16, add)

        def give(i):
            dev, qq = plane(offset(i))
            remote(s.at[qq], r1.at[offset(i)], s1, q1, dev).start()

        each(15, give)

    waiting = None
    for (at, width, _), (ks, direct, _, parts) in zip(PIECES, pieces):
        for b in range(IMG):
            pre = dot(left[0, image(b), :], winT[:, ks]) + bias[:, at : at + width]
            cdf = 0.5 * (1.0 + lax.erf(pre * (1.0 / math.sqrt(2.0))))
            right[1, image(b), ks] = (pre * cdf).astype(BF16)
            slope = cdf + pre * jnp.exp(-0.5 * pre * pre) * (1.0 / math.sqrt(2.0 * math.pi))
            right[0, image(b), ks] = (ga[image(b), ks] * slope).astype(BF16)
        if waiting:
            scatter(*waiting)
        grads = parts[0]
        grads[other] = dot(flip[other], right[other, :, ks]).astype(BF16).reshape(16, 16, width)
        if not direct:
            start(remote(grads.at[other], parts[1], parts[6], parts[7], partner))
        grads[core] = dot(flip[core], right[core, :, ks]).astype(BF16).reshape(16, 16, width)
        waiting = direct, parts
    scatter(*waiting)

    by_gain = by_shift = None
    for b in range(IMG):
        v = dot(right[0, image(b), :], win[...]).astype(BF16)
        gn[image(b), :] = v
        v = v.astype(F32)
        along = v * xh[image(b), :]
        f_src[pl.ds(slot(0, b), 1), :] = jnp.sum(v * gcol[0], axis=0, keepdims=True)
        f_src[pl.ds(slot(1, b), 1), :] = jnp.sum(along * gcol[0], axis=0, keepdims=True)
        by_gain = along if b == 0 else by_gain + along
        by_shift = v if b == 0 else by_shift + v
    start(remote(f_src, f_in, fs.at[0], fq1, partner))

    db = dot(jnp.ones((8, ROWS), BF16), right[0])[0:1]
    for i in range(5):
        small[pl.ds(i, 1), :] = db[:, i * 128 : i * 128 + 128]
    ones = jnp.ones((8, PATCH), BF16)
    for i, v in enumerate((by_gain, by_shift)):
        hi = v.astype(BF16)
        rest = v - hi.astype(F32)
        mid = rest.astype(BF16)
        low = (rest - mid.astype(F32)).astype(BF16)
        one = (dot_nt(ones, hi) + dot_nt(ones, mid) + dot_nt(ones, low))[0:1]
        small[pl.ds(5 + i, 1), :] = one[:, :128]
        small[pl.ds(7, 1), pl.ds(32 * i, 32)] = one[:, 128:]
    small[pl.ds(7, 1), pl.ds(64, 64)] = jnp.zeros((1, 64), F32)
    each(15, lambda i: remote(small, sm1.at[offset(i)], a1, b1, plane(offset(i))[0]).start())

    second_step(f_src, f_in, f_sum, f_far, fq1, fs, fq2)

    for _, direct, _, parts in pieces:
        if direct:
            grads, r1, t, r2, _, q1, s2, q2, *_ = parts
            arrived(r1.at[pl.ds(1, 31)], q1)
            acc = grads[core, q].astype(F32)
        else:
            _, _, s, r1, t, r2, _, _, _, q1, s2, q2, *_ = parts
            arrived(r1.at[pl.ds(1, 15)], q1)
            acc = s[q].astype(F32)
        t[...] = lax.fori_loop(1, r1.shape[0], lambda j, a: a + r1[j].astype(F32), acc).astype(BF16)
        each(7, lambda i: remote(t, r2.at[hop(i)], s2, q2, column(hop(i))).start())

    moment = finish(f_sum, f_far, fq2)
    for b in range(IMG):
        inner = gn[image(b), :].astype(F32) * gcol[0] - moment(0, b) - xh[image(b), :] * moment(1, b)
        out_ref[image(b), :] = (left[1, image(b), :].astype(F32) + rs[pl.ds(b, 1), :] * inner).astype(BF16)

    arrived(sm1.at[pl.ds(1, 15)], b1)
    smt[...] = lax.fori_loop(1, 16, lambda j, a: a + sm1[j], small[...])
    each(7, lambda i: remote(smt, sm2.at[hop(i)], a2, b2, column(hop(i))).start())

    for _, direct, full, parts in pieces:
        t, r2, s2, q2, s3, q3 = parts[2:4] + parts[6:] if direct else parts[4:6] + parts[10:14]
        arrived(r2.at[pl.ds(1, 7)], q2)
        acc = lax.fori_loop(1, 8, lambda d, a: a + r2[d].astype(F32), t[...].astype(F32))
        full[core, q] = acc.astype(BF16)
        mine = full.at[core, q]

        def tell(i):
            remote(mine, mine, s3, q3, plane(offset(i))[0]).start()
            if direct:
                remote(mine, mine, s3, q3, plane(offset(i), other)[0]).start()

        each(15, tell)
        if direct:
            remote(mine, mine, s3, q3, partner).start()

    arrived(sm2.at[pl.ds(1, 7)], b2)
    near = smt[...] + sm2[7 - 6 * rem(z, 2)]
    sm3[...] = lax.fori_loop(1, 8, lambda d, a: a + sm2[d], smt[...])
    start(remote(sm3, sm4, a3, b3, partner))
    for _, direct, full, parts in pieces:
        if not direct:
            q3, s4, q4 = parts[13:]
            arrived(full.at[core, pl.ds(1, 15)], q3)
            remote(full.at[core], full.at[core], s4, q4, partner).start()
    arrived(sm4, b3)
    row = lax.broadcasted_iota(jnp.int32, (8, 128), 0)
    sum_ref[...] = jnp.where(row < 5, sm3[...] + sm4[...], near) * (1.0 / IMAGES)
    for _, direct, full, parts in pieces:
        if direct:
            grads, r1, t, r2, s1, q1, s2, q2, s3, q3 = parts
            r1 = r1.at[pl.ds(1, 31)]
            arrived(r1, q3)
            arrived(r1, s3)
        else:
            _, _, _, r1, _, r2, _, _, s1, _, s2, _, s3, _, s4, q4 = parts
            r1 = r1.at[pl.ds(1, 15)]
            arrived(full.at[other], q4)
            arrived(r1, s3)
            arrived(full.at[core], s4)
        arrived(r1, s1)
        arrived(r2.at[pl.ds(1, 7)], s2)
    arrived(sm1.at[pl.ds(1, 15)], a1)
    arrived(sm2.at[pl.ds(1, 7)], a2)
    for c in sends:
        c.wait_send()


def last_kernel(d_ref, *refs):
    fulls, refs = refs[: len(PIECES)], refs[len(PIECES) :]
    sum_ref, out, dwin, dwout, db, gain, shift, v1, v2, v3, v4, v5, sem = refs
    copies = []

    def put(i, src, dst):
        c = pltpu.make_async_copy(src, dst, sem.at[i])
        c.start()
        copies.append(c)

    put(0, d_ref, out)
    for (at, width, _), full in zip(PIECES, fulls):
        v2[:, pl.ds(at, width)] = full[1].reshape(PATCH, width).astype(F32) * (1.0 / IMAGES)
    put(1, v2, dwout)
    for n, ((at, width, _), full) in enumerate(zip(PIECES, fulls)):
        rows = pl.ds(at, width)
        v1[rows, :] = jnp.transpose(full[0].reshape(PATCH, width).astype(F32)) * (1.0 / IMAGES)
        put(6 + n, v1.at[rows], dwin.at[rows])
    v3[...] = sum_ref[0:5, :].reshape(HID)
    put(3, v3, db)
    for i, (v, dst) in enumerate(((v4, gain), (v5, shift))):
        v[pl.ds(0, 128)] = sum_ref[5 + i, :]
        v[pl.ds(128, 32)] = sum_ref[7, 32 * i : 32 * i + 32]
        put(4 + i, v, dst)
    for c in copies:
        c.wait()


def buf(dtype, *shape):
    return pltpu.VMEM(shape, dtype)


def shards(patches, cotangent, w_in, b_in, w_out, gain, bias):
    dma = pltpu.SemaphoreType.DMA
    vmem = pl.BlockSpec(memory_space=pltpu.VMEM)
    hbm = pl.BlockSpec(memory_space=pltpu.HBM)

    def turned(v):
        return v.transpose(0, 2, 1).reshape(ROWS, PATCH)

    def piece(width, direct):
        halves = [buf(BF16, 16, 16, width), buf(BF16, 16, 16, width)]
        return [
            buf(BF16, 2, 16, 16, width),
            *([] if direct else halves),
            buf(BF16, 32 if direct else 16, 16, width),
            buf(BF16, 16, width),
            buf(BF16, 8, 16, width),
            *[dma] * (6 if direct else 10),
        ]

    d, *fulls, sums = pl.pallas_call(
        kernel,
        out_shape=(
            jax.ShapeDtypeStruct((ROWS, PATCH), BF16),
            *(jax.ShapeDtypeStruct((2, 16, 16, width), BF16) for _, width, _ in PIECES),
            jax.ShapeDtypeStruct((8, 128), F32),
        ),
        in_specs=[hbm] * 7,
        out_specs=(vmem,) * (2 + len(PIECES)),
        scratch_shapes=[
            buf(BF16, ROWS, PATCH),
            buf(BF16, HID, PATCH),
            buf(BF16, PATCH, HID),
            buf(BF16, PATCH, HID),
            buf(F32, HID),
            buf(F32, CHANNELS),
            buf(F32, CHANNELS),
            buf(F32, 5, 128),
            buf(F32, 10, 128),
            buf(BF16, 2, ROWS, PATCH),
            buf(BF16, 2, PATCH, ROWS),
            buf(BF16, 2, ROWS, HID),
            buf(F32, ROWS, HID),
            buf(F32, ROWS, PATCH),
            buf(F32, 8, PATCH),
            buf(BF16, ROWS, PATCH),
            buf(F32, 2, LOCAL, PATCH),
            buf(F32, 16, PATCH), buf(F32, 7, 16, PATCH),
            buf(F32, 16, PATCH), buf(F32, 16, PATCH), buf(F32, 2, 8, PATCH), buf(F32, 3, 2, 8, PATCH),
            buf(F32, 8, 128),
            buf(F32, 16, 8, 128), buf(F32, 8, 128), buf(F32, 8, 8, 128), buf(F32, 8, 128), buf(F32, 8, 128),
            dma((16,)), dma((7,)), dma, dma((7,)), dma, dma,
            dma, dma, dma, dma, dma, dma,
            *(v for _, width, direct in PIECES for v in piece(width, direct)),
        ],
        compiler_params=pltpu.CompilerParams(collective_id=0, has_side_effects=True, vmem_limit_bytes=40000000),
    )(
        *(
            pltpu.with_memory_space_constraint(v, pltpu.HBM)
            for v in (turned(patches), turned(cotangent), w_in, w_out, b_in, gain, bias)
        )
    )
    out, dwin, dwout, db, dgain, dshift = pl.pallas_call(
        last_kernel,
        out_shape=(
            jax.ShapeDtypeStruct((ROWS, PATCH), BF16),
            jax.ShapeDtypeStruct((HID, PATCH), F32),
            jax.ShapeDtypeStruct((PATCH, HID), F32),
            jax.ShapeDtypeStruct((HID,), F32),
            jax.ShapeDtypeStruct((LOCAL,), F32),
            jax.ShapeDtypeStruct((LOCAL,), F32),
        ),
        in_specs=[vmem] * (2 + len(PIECES)),
        out_specs=(hbm,) * 6,
        scratch_shapes=[
            buf(F32, HID, PATCH), buf(F32, PATCH, HID), buf(F32, HID), buf(F32, LOCAL), buf(F32, LOCAL), dma((6 + len(PIECES),)),
        ],
        compiler_params=pltpu.CompilerParams(vmem_limit_bytes=8 * 1024 * 1024),
    )(d, *fulls, sums)
    return out.reshape(IMG, LOCAL, PATCH).transpose(0, 2, 1), dwin, dwout, db, dgain, dshift


def solution(mesh):
    placed = (P("dp", None, "chan"), P("dp", None, "chan"), P(), P(), P(), P(), P())
    return jax.shard_map(
        shards,
        mesh=mesh,
        in_specs=placed,
        out_specs=(P("dp", None, "chan"), P(), P(), P(), P("chan"), P("chan")),
        check_vma=False,
    )
```

time: 42.8 us -> 41.3 us (0.965)
  Pallas kernels: 42.1 us -> 40.6 us
    pallas_call x1, Pallas kernels: 40.7 us -> 39.2 us  [shards(): pl.pallas_call(kernel, out_shape=(jax.ShapeDtypeStruct((ROWS, PATCH), BF1...]
where the time goes in v5:
time: 41.3 us; the launch traced here: 41.2 us
  Pallas kernels  40.6 us (98%)
  between operations  0.64 us (2%)
    pallas_call x1, Pallas kernels, shards(): pl.pallas_call(kernel, out_shape=(jax.ShapeDtypeStruct((ROWS, PATCH), BF1...  39.2 us
    pallas_call x1, Pallas kernels, shards(): pl.pallas_call(last_kernel, out_shape=(jax.ShapeDtypeStruct((ROWS, PATCH)...  1.34 us

profile of v5, /device:TPU:1, one launch (start us, length us, event | category | flops | bytes accessed | tf_op | source)
XLA Modules:
  0.0 41.2 jit_solution(7327850777915773617)
XLA Ops:
  0.6 39.2 %shard_map.118 = (bf16[1280,256]{1,0:T(8,128)(2,1)S(1)}, bf16[2,16,16,384]{3,2,1,0:T(8,128)(2,1)S(1)}, bf16[2,16,16,256]{3,2,1,0:T(8,128)(2,1)S(1)}, f32[8,128]{1,0:T(8,128)S(1)}) custom-call(bf16[1280,256]{1,0:T(8,128)(2,1)} %bitcast.9, bf16[1280,256]{1,0:T(8,128)(2,1)} %bitcast.10, bf16[640,256]{1,0:T(8,128)(2,1)} %win_hbm.1, bf16[256,640]{1,0:T(8,128)(2,1)} %wout_hbm.1, ...), custom_call_target="tpu_custom_call" | custom-call | tf_op jit(solution)/shard_map/pallas_call | solution.py:399
  39.9 1.3 %shard_map.119 = (bf16[1280,256]{1,0:T(8,128)(2,1)}, f32[640,256]{1,0:T(8,128)}, f32[256,640]{1,0:T(8,128)}, f32[640]{0:T(1024)}, f32[160]{0:T(256)}, /*index=5*/f32[160]{0:T(256)}) custom-call(bf16[1280,256]{1,0:T(8,128)(2,1)S(1)} %get-tuple-element.16.d_ref, bf16[2,16,16,384]{3,2,1,0:T(8,128)(2,1)S(1)} %get-tuple-element.17.refs_0_, ...), custom_call_target="tpu_custom_call" | custom-call | tf_op jit(solution)/shard_map/pallas_call | solution.py:441

commit v6 on v5

--- a/solution.py
+++ b/solution.py
@@ -145,11 +145,12 @@
     for b in range(IMG):
         x_loads[b].wait()
         v = xv[image(b), :].astype(F32)
-        e_src[pl.ds(b, 1), :] = jnp.sum(v, axis=0, keepdims=True)
-        e_src[pl.ds(8 + b, 1), :] = jnp.sum(v * v, axis=0, keepdims=True)
+        e_src[b // 4, pl.ds(b % 4, 1), :] = jnp.sum(v, axis=0, keepdims=True)
+        e_src[b // 4, pl.ds(4 + b % 4, 1), :] = jnp.sum(v * v, axis=0, keepdims=True)
     pl.semaphore_wait(barrier, 26)
-    for n, dev in enumerate(chan_peers()):
-        start(remote(e_src, e_far.at[n], es.at[n], eq, dev))
+    for h in range(2):
+        for n, dev in enumerate(chan_peers()):
+            start(remote(e_src.at[h], e_far.at[h, n], es.at[7 * h + n], eq.at[h], dev))
 
     def second_step(src, came, summed, far, sem1, send, sem2):
         arrived(came, sem1)
@@ -182,20 +183,32 @@
         ga[image(b), :] = dot(left[1, image(b), :], wout[...])
     flip[1] = jnp.transpose(left[1])
 
-    arrived(e_far, eq)
-    tot = e_src[...]
-    for n in range(7):
-        tot = tot + e_far[n]
-    tot = tot * (1.0 / CHANNELS)
-    means = tot[:8]
-    rs[...] = lax.rsqrt(tot[8:] - means * means + eps_norm)
     rows5[...] = bv[...].reshape(5, 128)
     bias = jnp.concatenate([rows5[i : i + 1, :] for i in range(5)], axis=1)
-    for b in range(IMG):
-        xhat = (xv[image(b), :].astype(F32) - means[b : b + 1, :]) * rs[pl.ds(b, 1), :]
-        xh[image(b), :] = xhat
-        normed = (xhat * gcol[0] + gcol[1]).astype(BF16)
-        left[0, image(b), :] = normed
+
+    def hidden(b, at, width):
+        ks = pl.ds(at, width)
+        pre = dot(left[0, image(b), :], winT[:, ks]) + bias[:, at : at + width]
+        cdf = 0.5 * (1.0 + lax.erf(pre * (1.0 / math.sqrt(2.0))))
+        right[1, image(b), ks] = (pre * cdf).astype(BF16)
+        slope = cdf + pre * jnp.exp(-0.5 * pre * pre) * (1.0 / math.sqrt(2.0 * math.pi))
+        right[0, image(b), ks] = (ga[image(b), ks] * slope).astype(BF16)
+
+    for h in range(2):
+        arrived(e_far.at[h], eq.at[h])
+        tot = e_src[h]
+        for n in range(7):
+            tot = tot + e_far[h, n]
+        tot = tot * (1.0 / CHANNELS)
+        means = tot[:4]
+        rstd = lax.rsqrt(tot[4:] - means * means + eps_norm)
+        rs[pl.ds(4 * h, 4), :] = rstd
+        for i in range(4):
+            b = 4 * h + i
+            xhat = (xv[image(b), :].astype(F32) - means[i : i + 1, :]) * rstd[i : i + 1, :]
+            xh[image(b), :] = xhat
+            left[0, image(b), :] = (xhat * gcol[0] + gcol[1]).astype(BF16)
+            hidden(b, *PIECES[0][:2])
     flip[0] = jnp.transpose(left[0])
 
     def scatter(direct, parts):
@@ -231,12 +244,9 @@
 
     waiting = None
     for (at, width, _), (ks, direct, _, parts) in zip(PIECES, pieces):
-        for b in range(IMG):
-            pre = dot(left[0, image(b), :], winT[:, ks]) + bias[:, at : at + width]
-            cdf = 0.5 * (1.0 + lax.erf(pre * (1.0 / math.sqrt(2.0))))
-            right[1, image(b), ks] = (pre * cdf).astype(BF16)
-            slope = cdf + pre * jnp.exp(-0.5 * pre * pre) * (1.0 / math.sqrt(2.0 * math.pi))
-            right[0, image(b), ks] = (ga[image(b), ks] * slope).astype(BF16)
+        if at:
+            for b in range(IMG):
+                hidden(b, at, width)
         if waiting:
             scatter(*waiting)
         grads = parts[0]
@@ -285,7 +295,7 @@
             _, _, s, r1, t, r2, _, _, _, q1, s2, q2, *_ = parts
             arrived(r1.at[pl.ds(1, 15)], q1)
             acc = s[q].astype(F32)
-        t[...] = lax.fori_loop(1, r1.shape[0], lambda j, a: a + r1[j].astype(F32), acc).astype(BF16)
+        t[...] = lax.fori_loop(1, r1.shape[0], lambda j, a: a + r1[j].astype(F32), acc, unroll=r1.shape[0] - 1).astype(BF16)
         each(7, lambda i: remote(t, r2.at[hop(i)], s2, q2, column(hop(i))).start())
 
     moment = finish(f_sum, f_far, fq2)
@@ -300,7 +310,7 @@
     for _, direct, full, parts in pieces:
         t, r2, s2, q2, s3, q3 = parts[2:4] + parts[6:] if direct else parts[4:6] + parts[10:14]
         arrived(r2.at[pl.ds(1, 7)], q2)
-        acc = lax.fori_loop(1, 8, lambda d, a: a + r2[d].astype(F32), t[...].astype(F32))
+        acc = lax.fori_loop(1, 8, lambda d, a: a + r2[d].astype(F32), t[...].astype(F32), unroll=7)
         full[core, q] = acc.astype(BF16)
         mine = full.at[core, q]
 
@@ -423,11 +433,11 @@
             buf(F32, 8, PATCH),
             buf(BF16, ROWS, PATCH),
             buf(F32, 2, LOCAL, PATCH),
-            buf(F32, 16, PATCH), buf(F32, 7, 16, PATCH),
+            buf(F32, 2, 8, PATCH), buf(F32, 2, 7, 8, PATCH),
             buf(F32, 16, PATCH), buf(F32, 16, PATCH), buf(F32, 2, 8, PATCH), buf(F32, 3, 2, 8, PATCH),
             buf(F32, 8, 128),
             buf(F32, 16, 8, 128), buf(F32, 8, 128), buf(F32, 8, 8, 128), buf(F32, 8, 128), buf(F32, 8, 128),
-            dma((16,)), dma((7,)), dma, dma((7,)), dma, dma,
+            dma((16,)), dma((14,)), dma((2,)), dma((7,)), dma, dma,
             dma, dma, dma, dma, dma, dma,
             *(v for _, width, direct in PIECES for v in piece(width, direct)),
         ],

time: 41.3 us -> 40.9 us (level)
  Pallas kernels: 40.6 us -> 40.1 us
    pallas_call x1, Pallas kernels: 39.2 us -> 38.8 us  [shards(): pl.pallas_call(kernel, out_shape=(jax.ShapeDtypeStruct((ROWS, PATCH), BF1...]
where the time goes in v6:
time: 40.9 us; the launch traced here: 40.8 us
  Pallas kernels  40.1 us (98%)
  between operations  0.64 us (2%)
    pallas_call x1, Pallas kernels, shards(): pl.pallas_call(kernel, out_shape=(jax.ShapeDtypeStruct((ROWS, PATCH), BF1...  38.8 us
    pallas_call x1, Pallas kernels, shards(): pl.pallas_call(last_kernel, out_shape=(jax.ShapeDtypeStruct((ROWS, PATCH)...  1.34 us

profile of v6, /device:TPU:1, one launch (start us, length us, event | category | flops | bytes accessed | tf_op | source)
XLA Modules:
  0.0 40.8 jit_solution(15141477492017541066)
XLA Ops:
  0.6 38.8 %shard_map.118 = (bf16[1280,256]{1,0:T(8,128)(2,1)S(1)}, bf16[2,16,16,384]{3,2,1,0:T(8,128)(2,1)S(1)}, bf16[2,16,16,256]{3,2,1,0:T(8,128)(2,1)S(1)}, f32[8,128]{1,0:T(8,128)S(1)}) custom-call(bf16[1280,256]{1,0:T(8,128)(2,1)} %bitcast.9, bf16[1280,256]{1,0:T(8,128)(2,1)} %bitcast.10, bf16[640,256]{1,0:T(8,128)(2,1)} %win_hbm.1, bf16[256,640]{1,0:T(8,128)(2,1)} %wout_hbm.1, ...), custom_call_target="tpu_custom_call" | custom-call | tf_op jit(solution)/shard_map/pallas_call | solution.py:409
  39.4 1.3 %shard_map.119 = (bf16[1280,256]{1,0:T(8,128)(2,1)}, f32[640,256]{1,0:T(8,128)}, f32[256,640]{1,0:T(8,128)}, f32[640]{0:T(1024)}, f32[160]{0:T(256)}, /*index=5*/f32[160]{0:T(256)}) custom-call(bf16[1280,256]{1,0:T(8,128)(2,1)S(1)} %get-tuple-element.16.d_ref, bf16[2,16,16,384]{3,2,1,0:T(8,128)(2,1)S(1)} %get-tuple-element.17.refs_0_, ...), custom_call_target="tpu_custom_call" | custom-call | tf_op jit(solution)/shard_map/pallas_call | solution.py:451

commit v7 on v6

--- a/solution.py
+++ b/solution.py
@@ -303,10 +303,6 @@
         inner = gn[image(b), :].astype(F32) * gcol[0] - moment(0, b) - xh[image(b), :] * moment(1, b)
         out_ref[image(b), :] = (left[1, image(b), :].astype(F32) + rs[pl.ds(b, 1), :] * inner).astype(BF16)
 
-    arrived(sm1.at[pl.ds(1, 15)], b1)
-    smt[...] = lax.fori_loop(1, 16, lambda j, a: a + sm1[j], small[...])
-    each(7, lambda i: remote(smt, sm2.at[hop(i)], a2, b2, column(hop(i))).start())
-
     for _, direct, full, parts in pieces:
         t, r2, s2, q2, s3, q3 = parts[2:4] + parts[6:] if direct else parts[4:6] + parts[10:14]
         arrived(r2.at[pl.ds(1, 7)], q2)
@@ -322,6 +318,10 @@
         each(15, tell)
         if direct:
             remote(mine, mine, s3, q3, partner).start()
+        else:
+            arrived(sm1.at[pl.ds(1, 15)], b1)
+            smt[...] = lax.fori_loop(1, 16, lambda j, a: a + sm1[j], small[...])
+            each(7, lambda i: remote(smt, sm2.at[hop(i)], a2, b2, column(hop(i))).start())
 
     arrived(sm2.at[pl.ds(1, 7)], b2)
     near = smt[...] + sm2[7 - 6 * rem(z, 2)]

time: 40.9 us -> 40.9 us (level)
  no operation moved by 1% of the time
where the time goes in v7:
time: 40.9 us; the launch traced here: 40.8 us
  Pallas kernels  40.1 us (98%)
  between operations  0.64 us (2%)
    pallas_call x1, Pallas kernels, shards(): pl.pallas_call(kernel, out_shape=(jax.ShapeDtypeStruct((ROWS, PATCH), BF1...  38.8 us
    pallas_call x1, Pallas kernels, shards(): pl.pallas_call(last_kernel, out_shape=(jax.ShapeDtypeStruct((ROWS, PATCH)...  1.34 us

profile of v7, /device:TPU:1, one launch (start us, length us, event | category | flops | bytes accessed | tf_op | source)
XLA Modules:
  0.0 40.8 jit_solution(5882608199527552710)
XLA Ops:
  0.6 38.8 %shard_map.118 = (bf16[1280,256]{1,0:T(8,128)(2,1)S(1)}, bf16[2,16,16,384]{3,2,1,0:T(8,128)(2,1)S(1)}, bf16[2,16,16,256]{3,2,1,0:T(8,128)(2,1)S(1)}, f32[8,128]{1,0:T(8,128)S(1)}) custom-call(bf16[1280,256]{1,0:T(8,128)(2,1)} %bitcast.9, bf16[1280,256]{1,0:T(8,128)(2,1)} %bitcast.10, bf16[640,256]{1,0:T(8,128)(2,1)} %win_hbm.1, bf16[256,640]{1,0:T(8,128)(2,1)} %wout_hbm.1, ...), custom_call_target="tpu_custom_call" | custom-call | tf_op jit(solution)/shard_map/pallas_call | solution.py:409
  39.4 1.3 %shard_map.119 = (bf16[1280,256]{1,0:T(8,128)(2,1)}, f32[640,256]{1,0:T(8,128)}, f32[256,640]{1,0:T(8,128)}, f32[640]{0:T(1024)}, f32[160]{0:T(256)}, /*index=5*/f32[160]{0:T(256)}) custom-call(bf16[1280,256]{1,0:T(8,128)(2,1)S(1)} %get-tuple-element.16.d_ref, bf16[2,16,16,384]{3,2,1,0:T(8,128)(2,1)S(1)} %get-tuple-element.17.refs_0_, ...), custom_call_target="tpu_custom_call" | custom-call | tf_op jit(solution)/shard_map/pallas_call | solution.py:451
